TPU v7x, 32 devices: a whole 2x2x4 slice. The times are simulated.
32 devices in a mesh: space: 4 (over y, x), sub: 8 (over z, core).
Axes of the slice: x: 2, y: 2, z: 4, core: 2. Of those that a mesh axis runs over, the one named last changes fastest.
Arguments:
- positions: float32 [3, 4, 512, 128], P(None, 'space', 'sub'), may hold values from 0 to 1.5
- masses: float32 [4, 512, 128], P('space', 'sub'), may hold values from 0.1 to 1
- occupancy: int32 [4, 512], P('space', 'sub'), may hold values from 1 to 128
- export_slots: int32 [4, 256], P('space', 'sub'), may hold values from 0 to 63, as said below
- export_count: int32 [4, 8], P('space', 'sub'), may hold values from 16 to 32
- pair_list: int32 [2, 4, 512], P(None, 'space', 'sub'), may hold values from 0 to 319, as said below
- pair_count: int32 [4, 8], P('space', 'sub'), may hold values from 16 to 64
Outputs:
- forces: float32 [3, 4, 512, 128], P(None, 'space', 'sub')
Inputs may be any that keep to these rules, and one draw needn't show every extreme that they name: `export_slots`: the 32 entries of one device are distinct own-leaf indices. `pair_list`: row 0 is a target own leaf, below 64; row 1 is a source pool leaf, below 320, never equal to the target.
All inputs are finite; a program needn't handle non-finite values.
Results may differ from a plain program's by a relative error of at most 0.0003.
Values sent between devices are 32-bit elements; how exact they have to be, the bound alone decides.
No kernel may reach another device: no remote copies, remote signals or barrier semaphores. Data moves between devices by JAX's collectives and lax.ppermute only.
A program may use at most 64 MiB of HBM per device.

v0:
```python
import functools

import jax
import jax.numpy as jnp
from jax import lax
from jax.experimental import pallas as pl
from jax.experimental.pallas import tpu as pltpu
from jax.sharding import PartitionSpec as P

OFFSETS = ((-1, -1), (-1, 0), (-1, 1), (0, -1), (0, 1), (1, -1), (1, 0), (1, 1))
LOCAL = 8
SOFTEN = 0.05
CENTER = 0.75
TABLE = 8
CODE = 1024
UNROLL = 8


def vmem():
    return pl.BlockSpec(memory_space=pltpu.VMEM)


def on_chip(value):
    return pltpu.with_memory_space_constraint(value, pltpu.VMEM)


def column(row, size):
    a = lax.broadcasted_iota(jnp.int32, (size, size), 0)
    b = lax.broadcasted_iota(jnp.int32, (size, size), 1)
    return jnp.sum(jnp.where(a == b, row[:, :size], 0), axis=1, keepdims=True)


def pack_kernel(pos, mass, occupancy, slots, count, pairs, pair_count, out, *, leaves, sent, slots_of_pairs):
    lanes = mass.shape[-1]
    occ = column(occupancy[...], leaves)
    lane = lax.broadcasted_iota(jnp.int32, (leaves, lanes), 1)
    live = jnp.where(lane < occ, mass[0], 0.0)
    for c in range(3):
        out[pl.ds(c, leaves, stride=4), :] = pos[c, 0] - CENTER
    out[pl.ds(3, leaves, stride=4), :] = live
    n = slots_of_pairs
    target = pairs[0]
    source = pairs[1]
    index = lax.broadcasted_iota(jnp.int32, (1, n), 1)
    key = jnp.where(source < leaves, LOCAL, (source - leaves) // sent)
    key = jnp.where(index < pair_count[0, 0], key, LOCAL + 1)
    code = target * CODE + source
    order = key * CODE + index
    order_col = column(order, n)
    code_col = column(code, n)
    rank = jnp.sum((order < order_col).astype(jnp.int32), axis=1, keepdims=True)
    place = lax.broadcasted_iota(jnp.int32, (n, lanes), 1)
    sorted_code = jnp.sum(jnp.where(place == rank, code_col, 0), axis=0, keepdims=True)
    starts = jnp.sum((order_col < place * CODE).astype(jnp.int32), axis=0, keepdims=True)
    g = lax.broadcasted_iota(jnp.int32, (1, sent), 1)
    alive = jnp.where(g < count[0, 0], slots[...], -1)
    base = 4 * leaves
    out[pl.ds(base, TABLE), :] = jnp.zeros((TABLE, lanes), jnp.float32)
    out[pl.ds(base, 1), :] = sorted_code.astype(jnp.float32)
    out[pl.ds(base + 1, 1), :] = starts.astype(jnp.float32)
    out[pl.ds(base + 2, 1), :sent] = alive.astype(jnp.float32)


def split3(a):
    a1 = a.astype(jnp.bfloat16).astype(jnp.float32)
    r = a - a1
    a2 = r.astype(jnp.bfloat16).astype(jnp.float32)
    return a1, a2, r - a2


def features(target, source):
    row = lax.broadcasted_iota(jnp.int32, source.shape, 0)
    xs = jnp.where(row < 3, source, 0.0)
    xt = jnp.where(row < 3, target, 0.0)
    ms = source[3:4]
    qs = jnp.sum(xs * xs, axis=0, keepdims=True) + SOFTEN
    qt = jnp.sum(xt * xt, axis=0, keepdims=True)
    a = jnp.where(row < 3, -2.0 * xs, jnp.where(row == 3, qs, jnp.where(row == 4, 1.0, 0.0)))
    b = jnp.where(row < 3, xt, jnp.where(row == 3, 1.0, jnp.where(row == 4, qt, 0.0)))
    g = jnp.where(row < 3, xs * ms, jnp.where(row == 3, ms, 0.0))
    a1, a2, a3 = split3(a)
    b1, b2, b3 = split3(b)
    g1, g2, g3 = split3(g)
    left = jnp.concatenate([a1, a1, a2, a2, a1, a3], axis=0).astype(jnp.bfloat16)
    right = jnp.concatenate([b1, b2, b1, b2, b3, b1], axis=0).astype(jnp.bfloat16)
    moments = jnp.concatenate([g1 + pltpu.roll(g2, 4, 0), g3], axis=0).astype(jnp.bfloat16)
    return left, right, moments


def moment_sums(softened, moments):
    inverse = lax.rsqrt(softened)
    scaled = jnp.maximum((1.0 + SOFTEN) - softened, 0.0) * inverse
    weight = scaled * scaled * inverse
    high = weight.astype(jnp.bfloat16)
    low = (weight - high.astype(jnp.float32)).astype(jnp.bfloat16)
    total = jnp.dot(moments, high, preferred_element_type=jnp.float32)
    total = total + jnp.dot(moments, low, preferred_element_type=jnp.float32)
    return total[:8] + total[8:]


def run_list(targets, sources, total, own, pool, acc, squares, weights):
    lanes = own.shape[1]
    squares[...] = jnp.full(squares.shape, 2.0, jnp.float32)
    weights[...] = jnp.zeros(weights.shape, jnp.bfloat16)

    def finish(base):
        sums = []
        for u in range(UNROLL):
            sums.append(moment_sums(squares[pl.ds(u * lanes, lanes), :], weights[pl.ds(16 * u, 16), :]))
        return sums

    def add(base, sums):
        for u in range(UNROLL):
            at = pl.ds(pl.multiple_of(targets[base + u] * 8, 8), 8)
            acc[at, :] += sums[u]

    def step(i, carry):
        base = i * UNROLL
        sums = finish(base)
        for u in range(UNROLL):
            t = targets[base + UNROLL + u]
            s = sources[base + UNROLL + u]
            left, right, moments = features(own[pl.ds(4 * t, 8), :], pool[pl.ds(s, 8), :])
            squares[pl.ds(u * lanes, lanes), :] = lax.dot_general(
                left, right, (((0,), (0,)), ((), ())), preferred_element_type=jnp.float32
            )
            weights[pl.ds(16 * u, 16), :] = moments
        add(base, sums)
        return carry

    steps = (total - 1) // UNROLL
    lax.fori_loop(0, steps, step, 0)
    add(steps * UNROLL, finish(steps * UNROLL))


def open_list(targets, sources, null_row):
    for u in range(UNROLL):
        targets[u] = 0
        sources[u] = null_row


def close_list(targets, sources, total, null_row):
    for u in range(UNROLL):
        targets[total + u] = 0
        sources[total + u] = null_row


def fetch_tables(packed, staging, tables, sem):
    for n, (ref, row) in enumerate(packed):
        staging[n] = ref[pl.ds(row, TABLE), :].astype(jnp.int32)
    copy = pltpu.make_async_copy(staging, tables, sem)
    copy.start()
    copy.wait()


def local_kernel(own, acc, staging, tables, targets, sources, squares, weights, sem, *, leaves):
    rows = 4 * leaves
    acc[...] = jnp.zeros_like(acc)
    fetch_tables([(own, rows)], staging, tables, sem)
    open_list(targets, sources, rows)

    def itself(i, carry):
        targets[UNROLL + i] = i
        sources[UNROLL + i] = 4 * i
        return carry

    lax.fori_loop(0, leaves, itself, 0)

    def both(j, n):
        code = tables[0, 0, j]
        t = code // CODE
        u = code % CODE
        targets[n] = t
        sources[n] = 4 * u
        targets[n + 1] = u
        sources[n + 1] = 4 * t
        return n + 2

    total = lax.fori_loop(tables[0, 1, LOCAL], tables[0, 1, LOCAL + 1], both, UNROLL + leaves)
    close_list(targets, sources, total, rows)
    run_list(targets, sources, total, own, own, acc, squares, weights)


def ghost_list(tables, offsets, targets, sources, stride, leaves, sent):
    total = jnp.int32(UNROLL)
    for n, k in enumerate(offsets):
        row0 = n * stride

        def mine(j, total, n=n, k=k, row0=row0):
            code = tables[0, 0, j]
            leaf = tables[1 + n, 2, code % CODE - (leaves + k * sent)]
            targets[total] = code // CODE
            sources[total] = row0 + 4 * leaf
            return total + (leaf >= 0).astype(jnp.int32)

        total = lax.fori_loop(tables[0, 1, k], tables[0, 1, k + 1], mine, total)
        back = 7 - k

        def theirs(j, total, n=n, back=back, row0=row0):
            code = tables[1 + n, 0, j]
            leaf = tables[0, 2, code % CODE - (leaves + back * sent)]
            targets[total] = leaf
            sources[total] = row0 + 4 * (code // CODE)
            return total + (leaf >= 0).astype(jnp.int32)

        total = lax.fori_loop(tables[1 + n, 1, back], tables[1 + n, 1, back + 1], theirs, total)
    return total


def ghost_body(own, parts, acc_in, acc, pool, staging, tables, targets, sources, squares, weights, sem, offsets, leaves, sent):
    rows = 4 * leaves
    stride = rows + TABLE
    fetch_tables([(own, rows)] + [(ref, row + rows) for ref, row in parts], staging, tables, sem)
    for n, (ref, row) in enumerate(parts):
        pool[pl.ds(n * stride, stride), :] = ref[pl.ds(row, stride), :]
    open_list(targets, sources, rows)
    total = ghost_list(tables, offsets, targets, sources, stride, leaves, sent)
    close_list(targets, sources, total, rows)
    run_list(targets, sources, total, own, pool, acc, squares, weights)


def face_kernel(own, p1, p3, p4, p6, acc_in, acc, pool, staging, tables, targets, sources, squares, weights, sem, *, leaves, sent):
    acc[...] = acc_in[...]
    parts = [(p1, 0), (p3, 0), (p4, 0), (p6, 0)]
    ghost_body(own, parts, acc_in, acc, pool, staging, tables, targets, sources, squares, weights, sem, (1, 3, 4, 6), leaves, sent)


def corner_kernel(own, lower, upper, acc_in, out, acc, pool, staging, tables, targets, sources, squares, weights, sem, *, leaves, sent):
    stride = 4 * leaves + TABLE
    acc[...] = acc_in[...]
    parts = [(lower, 0), (lower, stride), (upper, 0), (upper, stride)]
    ghost_body(own, parts, acc_in, acc, pool, staging, tables, targets, sources, squares, weights, sem, (0, 5, 2, 7), leaves, sent)

    def part(c):
        return acc[pl.ds(c, leaves, stride=8), :] + acc[pl.ds(c + 4, leaves, stride=8), :]

    mass = own[pl.ds(3, leaves, stride=4), :]
    norm = part(3)
    for c in range(3):
        out[c, 0] = mass * (part(c) - own[pl.ds(c, leaves, stride=4), :] * norm)


def ring(size, step):
    return [(i, (i + step) % size) for i in range(size)]


def both_ways(value, axis):
    size = lax.axis_size(axis)
    return (lax.ppermute(value, axis, ring(size, 1)), lax.ppermute(value, axis, ring(size, -1)))


def local(positions, masses, occupancy, export_slots, export_count, pair_list, pair_count):
    leaves, lanes = masses.shape[1:]
    sent = export_slots.shape[1]
    slots_of_pairs = pair_list.shape[2]
    rows = 4 * leaves + TABLE
    f32 = jnp.float32
    smem = pl.BlockSpec(memory_space=pltpu.SMEM)
    packed = pl.pallas_call(
        functools.partial(pack_kernel, leaves=leaves, sent=sent, slots_of_pairs=slots_of_pairs),
        out_shape=pltpu.VMEM((rows, lanes), f32),
        in_specs=[vmem(), vmem(), vmem(), vmem(), smem, vmem(), smem],
        out_specs=vmem(),
        name="pack",
    )(positions, masses, occupancy, export_slots, export_count, pair_list, pair_count)

    def lists(tables, entries):
        return [
            pltpu.VMEM((tables, TABLE, lanes), jnp.int32),
            pltpu.SMEM((tables, TABLE, lanes), jnp.int32),
            pltpu.SMEM((entries + 2 * UNROLL,), jnp.int32),
            pltpu.SMEM((entries + 2 * UNROLL,), jnp.int32),
            pltpu.VMEM((UNROLL * lanes, lanes), f32),
            pltpu.VMEM((UNROLL * 16, lanes), jnp.bfloat16),
            pltpu.SemaphoreType.DMA,
        ]

    def cost(blocks):
        return pl.CostEstimate(flops=blocks * lanes * lanes * 200, transcendentals=0, bytes_accessed=rows * lanes * 4)

    accumulator = pltpu.VMEM((8 * leaves, lanes), f32)
    lower_s, upper_s = both_ways(packed, "space")
    lower_r, upper_r = both_ways(packed, "sub")
    acc = pl.pallas_call(
        functools.partial(local_kernel, leaves=leaves),
        out_shape=accumulator,
        in_specs=[vmem()],
        out_specs=vmem(),
        scratch_shapes=lists(1, leaves + 2 * slots_of_pairs),
        cost_estimate=cost(leaves + slots_of_pairs),
        name="own",
    )(on_chip(packed))
    corners = jnp.concatenate([lower_s, upper_s], axis=0)
    lower_c, upper_c = both_ways(corners, "sub")
    acc = pl.pallas_call(
        functools.partial(face_kernel, leaves=leaves, sent=sent),
        out_shape=accumulator,
        in_specs=[vmem()] * 6,
        out_specs=vmem(),
        scratch_shapes=[pltpu.VMEM((4 * rows, lanes), f32)] + lists(5, 5 * slots_of_pairs),
        cost_estimate=cost(slots_of_pairs),
        name="faces",
    )(*map(on_chip, (packed, lower_s, lower_r, upper_r, upper_s, acc)))
    return pl.pallas_call(
        functools.partial(corner_kernel, leaves=leaves, sent=sent),
        out_shape=jax.ShapeDtypeStruct((3, 1, leaves, lanes), f32),
        in_specs=[vmem()] * 4,
        out_specs=vmem(),
        scratch_shapes=[pltpu.VMEM((8 * leaves, lanes), f32), pltpu.VMEM((4 * rows, lanes), f32)]
        + lists(5, 5 * slots_of_pairs),
        cost_estimate=cost(slots_of_pairs),
        name="corners",
    )(*map(on_chip, (packed, lower_c, upper_c, acc)))


def solution(mesh):
    return jax.shard_map(
        local,
        mesh=mesh,
        in_specs=(
            P(None, "space", "sub", None),
            P("space", "sub", None),
            P("space", "sub"),
            P("space", "sub"),
            P("space", "sub"),
            P(None, "space", "sub"),
            P("space", "sub"),
        ),
        out_specs=P(None, "space", "sub", None),
        check_vma=False,
    )
```

profile of v0, /device:TPU:0, one launch (start us, length us, event | category | flops | bytes accessed | tf_op | source)
XLA Modules:
  0.0 35.1 jit_solution(8725885785902579044)
XLA Ops:
  1.3 1.1 %pack.1.own = f32[264,128]{1,0:T(8,128)S(1)} custom-call(f32[3,1,64,128]{3,2,1,0:T(8,128)} %pos.1, f32[1,64,128]{2,1,0:T(8,128)} %mass.1, s32[1,64]{1,0:T(1,128)} %occupancy.1, s32[1,32]{1,0:T(1,128)} %slots.1, s32[1,1]{1,0:T(1,128)S(6)} %copy.9.count, s32[2,1,64]{2,1,0:T(1,128)} %pairs.1, s32[1,1]{1,0:T(1,128)S(6)} %copy.10.pair_count), custom_call_target="tpu_custom_call" | custom-call | tf_op jit(solution)/shard_map/pack/pallas_call | solution.py:259
  2.5 3.0 %collective-permute-start = (f32[264,128]{1,0:T(8,128)S(1)}, f32[264,128]{1,0:T(8,128)S(1)}, u32[]{:S(2)}, u32[]{:S(2)}) collective-permute-start(f32[264,128]{1,0:T(8,128)S(1)} %pack.1.own), channel_id=1, source_target_pairs={{0,8},{8,16},{16,24},{24,0},{1,9},{9,17},{17,25},{25,1},{2,10},{10... | collective-permute-start | bytes 405512 | tf_op jit(solution)/shard_map/ppermute | solution.py:249
  5.5 1.0 %collective-permute-start.1 = (f32[264,128]{1,0:T(8,128)S(1)}, f32[264,128]{1,0:T(8,128)S(1)}, u32[]{:S(2)}, u32[]{:S(2)}) collective-permute-start(f32[264,128]{1,0:T(8,128)S(1)} %pack.1.own), channel_id=1, source_target_pairs={{0,24},{8,0},{16,8},{24,16},{1,25},{9,1},{17,9},{25,17},{2,26},{10... | collective-permute-start | bytes 405512 | tf_op jit(solution)/shard_map/ppermute | solution.py:249
  6.5 4.4 %collective-permute-done.p1 = f32[264,128]{1,0:T(8,128)S(1)} collective-permute-done((f32[264,128]{1,0:T(8,128)S(1)}, f32[264,128]{1,0:T(8,128)S(1)}, u32[]{:S(2)}, u32[]{:S(2)}) %collective-permute-start) | collective-permute-done | bytes 135200 | tf_op jit(solution)/shard_map/ppermute | solution.py:249
  10.9 2.3 %collective-permute-done.1.p6 = f32[264,128]{1,0:T(8,128)S(1)} collective-permute-done((f32[264,128]{1,0:T(8,128)S(1)}, f32[264,128]{1,0:T(8,128)S(1)}, u32[]{:S(2)}, u32[]{:S(2)}) %collective-permute-start.1) | collective-permute-done | bytes 135200 | tf_op jit(solution)/shard_map/ppermute | solution.py:249
  13.2 2.2 %collective-permute-start.3 = (f32[528,128]{1,0:T(8,128)S(1)}, f32[528,128]{1,0:T(8,128)S(1)}, u32[]{:S(2)}, u32[]{:S(2)}) collective-permute-start(f32[528,128]{1,0:T(8,128)S(1)} %constant_dynamic-update-slice_fusion), channel_id=1, source_target_pairs={{0,7},{1,0},{2,1},{3,2},{4,3},{5,4},{6,5},{7,6},{8,15},{9,8},{10,9... | collective-permute-start | bytes 811016 | tf_op jit(solution)/shard_map/ppermute | solution.py:249
  15.4 0.0 collective-permute-start.2
  15.4 3.5 %collective-permute-start.5 = (f32[264,128]{1,0:T(8,128)S(1)}, f32[264,128]{1,0:T(8,128)S(1)}, u32[]{:S(2)}, u32[]{:S(2)}) collective-permute-start(f32[264,128]{1,0:T(8,128)S(1)} %pack.1.own), channel_id=1, source_target_pairs={{0,7},{1,0},{2,1},{3,2},{4,3},{5,4},{6,5},{7,6},{8,15},{9,8},{10,9... | collective-permute-start | bytes 405512 | tf_op jit(solution)/shard_map/ppermute | solution.py:249
  19.0 0.0 collective-permute-start.4
  19.0 5.9 %own.1.acc_in = f32[512,128]{1,0:T(8,128)S(1)} custom-call(f32[264,128]{1,0:T(8,128)S(1)} %pack.1.own), custom_call_target="tpu_custom_call" | custom-call | flops 419430400 | bytes 135168 | tf_op jit(solution)/shard_map/own/pallas_call | solution.py:284
  24.9 0.0 collective-permute-done.5.p4
  24.9 2.1 %collective-permute-done.4.p3 = f32[264,128]{1,0:T(8,128)S(1)} collective-permute-done((f32[264,128]{1,0:T(8,128)S(1)}, f32[264,128]{1,0:T(8,128)S(1)}, u32[]{:S(2)}, u32[]{:S(2)}) %collective-permute-start.4) | collective-permute-done | bytes 135200 | tf_op jit(solution)/shard_map/ppermute | solution.py:249
  27.1 3.6 %faces.1.acc_in = f32[512,128]{1,0:T(8,128)S(1)} custom-call(f32[264,128]{1,0:T(8,128)S(1)} %pack.1.own, f32[264,128]{1,0:T(8,128)S(1)} %collective-permute-done.p1, f32[264,128]{1,0:T(8,128)S(1)} %collective-permute-done.4.p3, f32[264,128]{1,0:T(8,128)S(1)} %collective-permute-done.5.p4, f32[264,128]{1,0:T(8,128)S(1)} %collective-permute-done.1.p6, ...), custom_call_target="tpu_custom_call" | custom-call | flops 209715200 | bytes 135168 | tf_op jit(solution)/shard_map/faces/pallas_call | solution.py:295
  30.7 0.0 collective-permute-done.3.upper
  30.7 0.0 collective-permute-done.2.lower
  30.7 4.4 %corners.1 = f32[3,1,64,128]{3,2,1,0:T(8,128)} custom-call(f32[264,128]{1,0:T(8,128)S(1)} %pack.1.own, f32[528,128]{1,0:T(8,128)S(1)} %collective-permute-done.2.lower, f32[528,128]{1,0:T(8,128)S(1)} %collective-permute-done.3.upper, f32[512,128]{1,0:T(8,128)S(1)} %faces.1.acc_in), custom_call_target="tpu_custom_call" | custom-call | flops 209715200 | bytes 135168 | tf_op jit(solution)/shard_map/corners/pallas_call | solution.py:304
  (2 shorter events, 0.0 us)
Async XLA Ops:
  2.5 8.4 %collective-permute-start = (f32[264,128]{1,0:T(8,128)S(1)}, f32[264,128]{1,0:T(8,128)S(1)}, u32[]{:S(2)}, u32[]{:S(2)}) collective-permute-start(f32[264,128]{1,0:T(8,128)S(1)} %pack.1.own), channel_id=1, source_target_pairs={{0,8},{8,16},{16,24},{24,0},{1,9},{9,17},{17,25},{25,1},{2,10},{10... | collective-permute-start | bytes 405512 | tf_op jit(solution)/shard_map/ppermute | solution.py:249
  5.5 7.7 %collective-permute-start.1 = (f32[264,128]{1,0:T(8,128)S(1)}, f32[264,128]{1,0:T(8,128)S(1)}, u32[]{:S(2)}, u32[]{:S(2)}) collective-permute-start(f32[264,128]{1,0:T(8,128)S(1)} %pack.1.own), channel_id=1, source_target_pairs={{0,24},{8,0},{16,8},{24,16},{1,25},{9,1},{17,9},{25,17},{2,26},{10... | collective-permute-start | bytes 405512 | tf_op jit(solution)/shard_map/ppermute | solution.py:249
  13.2 17.5 %collective-permute-start.3 = (f32[528,128]{1,0:T(8,128)S(1)}, f32[528,128]{1,0:T(8,128)S(1)}, u32[]{:S(2)}, u32[]{:S(2)}) collective-permute-start(f32[528,128]{1,0:T(8,128)S(1)} %constant_dynamic-update-slice_fusion), channel_id=1, source_target_pairs={{0,7},{1,0},{2,1},{3,2},{4,3},{5,4},{6,5},{7,6},{8,15},{9,8},{10,9... | collective-permute-start | bytes 811016 | tf_op jit(solution)/shard_map/ppermute | solution.py:249
  15.4 15.3 %collective-permute-start.2 = (f32[528,128]{1,0:T(8,128)S(1)}, f32[528,128]{1,0:T(8,128)S(1)}, u32[]{:S(2)}, u32[]{:S(2)}) collective-permute-start(f32[528,128]{1,0:T(8,128)S(1)} %constant_dynamic-update-slice_fusion), channel_id=1, source_target_pairs={{0,1},{1,2},{2,3},{3,4},{4,5},{5,6},{6,7},{7,0},{8,9},{9,10},{10,1... | collective-permute-start | bytes 811016 | tf_op jit(solution)/shard_map/ppermute | solution.py:249
  15.4 9.5 %collective-permute-start.5 = (f32[264,128]{1,0:T(8,128)S(1)}, f32[264,128]{1,0:T(8,128)S(1)}, u32[]{:S(2)}, u32[]{:S(2)}) collective-permute-start(f32[264,128]{1,0:T(8,128)S(1)} %pack.1.own), channel_id=1, source_target_pairs={{0,7},{1,0},{2,1},{3,2},{4,3},{5,4},{6,5},{7,6},{8,15},{9,8},{10,9... | collective-permute-start | bytes 405512 | tf_op jit(solution)/shard_map/ppermute | solution.py:249
  19.0 8.1 %collective-permute-start.4 = (f32[264,128]{1,0:T(8,128)S(1)}, f32[264,128]{1,0:T(8,128)S(1)}, u32[]{:S(2)}, u32[]{:S(2)}) collective-permute-start(f32[264,128]{1,0:T(8,128)S(1)} %pack.1.own), channel_id=1, source_target_pairs={{0,1},{1,2},{2,3},{3,4},{4,5},{5,6},{6,7},{7,0},{8,9},{9,10},{10,1... | collective-permute-start | bytes 405512 | tf_op jit(solution)/shard_map/ppermute | solution.py:249
where the time goes:
time: 34.8 us; the launch traced here: 35.1 us
  Pallas kernels  15.1 us (43%)
  starting transfers between devices  9.83 us (28%)
  waiting for transfers between devices  8.81 us (25%)
  between operations  1.36 us (4%)
    ppermute x3, starting transfers between devices, both_ways(): lax.ppermute(value, axis, ring(size, -1))  6.8 us
    ppermute x3, waiting for transfers between devices, both_ways(): lax.ppermute(value, axis, ring(size, 1))  6.52 us
    pallas_call x1, Pallas kernels, local(): pl.pallas_call(functools.partial(local_kernel, leaves=leaves), out_shape=...  5.93 us
    pallas_call x1, Pallas kernels, local(): pl.pallas_call(functools.partial(corner_kernel, leaves=leaves, sent=sent)...  4.4 us
    pallas_call x1, Pallas kernels, local(): pl.pallas_call(functools.partial(face_kernel, leaves=leaves, sent=sent),...  3.61 us
    ppermute x3, starting transfers between devices, both_ways(): lax.ppermute(value, axis, ring(size, 1))  3.02 us
    ppermute x3, waiting for transfers between devices, both_ways(): lax.ppermute(value, axis, ring(size, -1))  2.29 us
    pallas_call x1, Pallas kernels, local(): pl.pallas_call(functools.partial(pack_kernel, leaves=leaves, sent=sent, s...  1.15 us
  transfers between devices with their start and end apart: 6, of which 3 were waited for; matrix products, arithmetic and copies ran while one was open for 0% of the time, Pallas kernels for 27%

commit v1 on v0

v1 whole, which is shorter than its diff:
```python
import functools

import jax
import jax.numpy as jnp
from jax import lax
from jax.experimental import pallas as pl
from jax.experimental.pallas import tpu as pltpu
from jax.sharding import PartitionSpec as P


LOCAL = 8
SOFTEN = 0.05
CENTER = 0.75
TABLE = 8
CODE = 1024
BATCH = 8
CHUNK = 4


def vmem():
    return pl.BlockSpec(memory_space=pltpu.VMEM)


def on_chip(value):
    return pltpu.with_memory_space_constraint(value, pltpu.VMEM)


def column(row, size):
    a = lax.broadcasted_iota(jnp.int32, (size, size), 0)
    b = lax.broadcasted_iota(jnp.int32, (size, size), 1)
    return jnp.sum(jnp.where(a == b, row[:, :size], 0), axis=1, keepdims=True)


def pack_kernel(pos, mass, occupancy, slots, count, pairs, pair_count, out, *, leaves, sent, slots_of_pairs):
    lanes = mass.shape[-1]
    occ = column(occupancy[...], leaves)
    lane = lax.broadcasted_iota(jnp.int32, (leaves, lanes), 1)
    live = jnp.where(lane < occ, mass[0], 0.0)
    for c in range(3):
        out[pl.ds(c, leaves, stride=4), :] = pos[c, 0] - CENTER
    out[pl.ds(3, leaves, stride=4), :] = live
    n = slots_of_pairs
    target = pairs[0]
    source = pairs[1]
    index = lax.broadcasted_iota(jnp.int32, (1, n), 1)
    key = jnp.where(source < leaves, LOCAL, (source - leaves) // sent)
    key = jnp.where(index < pair_count[0, 0], key, LOCAL + 1)
    code = target * CODE + source
    order = key * CODE + index
    order_col = column(order, n)
    code_col = column(code, n)
    rank = jnp.sum((order < order_col).astype(jnp.int32), axis=1, keepdims=True)
    place = lax.broadcasted_iota(jnp.int32, (n, lanes), 1)
    sorted_code = jnp.sum(jnp.where(place == rank, code_col, 0), axis=0, keepdims=True)
    starts = jnp.sum((order_col < place * CODE).astype(jnp.int32), axis=0, keepdims=True)
    g = lax.broadcasted_iota(jnp.int32, (1, sent), 1)
    alive = jnp.where(g < count[0, 0], slots[...], -1)
    base = 4 * leaves
    out[pl.ds(base, TABLE), :] = jnp.zeros((TABLE, lanes), jnp.float32)
    out[pl.ds(base, 1), :] = sorted_code.astype(jnp.float32)
    out[pl.ds(base + 1, 1), :] = starts.astype(jnp.float32)
    out[pl.ds(base + 2, 1), :sent] = alive.astype(jnp.float32)


def split3(a):
    a1 = a.astype(jnp.bfloat16).astype(jnp.float32)
    r = a - a1
    a2 = r.astype(jnp.bfloat16).astype(jnp.float32)
    return a1, a2, r - a2


def features(target, source):
    row = lax.broadcasted_iota(jnp.int32, source.shape, 0)
    xs = jnp.where(row < 3, source, 0.0)
    xt = jnp.where(row < 3, target, 0.0)
    ms = source[3:4]
    qs = jnp.sum(xs * xs, axis=0, keepdims=True) + SOFTEN
    qt = jnp.sum(xt * xt, axis=0, keepdims=True)
    a = jnp.where(row < 3, -2.0 * xs, jnp.where(row == 3, qs, jnp.where(row == 4, 1.0, 0.0)))
    b = jnp.where(row < 3, xt, jnp.where(row == 3, 1.0, jnp.where(row == 4, qt, 0.0)))
    g = jnp.where(row < 3, xs * ms, jnp.where(row == 3, ms, 0.0))
    a1, a2, a3 = split3(a)
    b1, b2, b3 = split3(b)
    g1, g2, g3 = split3(g)
    left = jnp.concatenate([a1, a1, a2, a2, a1, a3], axis=0).astype(jnp.bfloat16)
    right = jnp.concatenate([b1, b2, b1, b2, b3, b1], axis=0).astype(jnp.bfloat16)
    moments = jnp.concatenate([g1 + pltpu.roll(g2, 4, 0), g3], axis=0).astype(jnp.bfloat16)
    return left, right, moments


def moment_sums(softened, moments):
    lanes = softened.shape[1] // 2
    inverse = lax.rsqrt(softened)
    scaled = jnp.maximum((1.0 + SOFTEN) - softened, 0.0) * inverse
    weight = scaled * scaled * inverse
    high = weight.astype(jnp.bfloat16)
    low = (weight - high.astype(jnp.float32)).astype(jnp.bfloat16)
    total = jnp.dot(
        jnp.concatenate([moments, moments], axis=1),
        jnp.concatenate([high, low], axis=0),
        preferred_element_type=jnp.float32,
    )
    return (
        total[0:8, :lanes] + total[8:16, :lanes],
        total[16:24, lanes:] + total[24:32, lanes:],
    )


def run_pairs(batches, first, second, own, pool, acc, squares, weights):
    lanes = own.shape[1]
    none = jnp.zeros((48, lanes), jnp.bfloat16)

    def begin(i):
        for u in range(0, BATCH, 2):
            sides = [
                features(own[pl.ds(4 * first(i, v), 8), :], pool[pl.ds(second(i, v), 8), :]) for v in (u, u + 1)
            ]
            left = jnp.concatenate([sides[0][0], sides[1][0]], axis=0)
            right = jnp.concatenate(
                [
                    jnp.concatenate([sides[0][1], none], axis=1),
                    jnp.concatenate([none, sides[1][1]], axis=1),
                ],
                axis=0,
            )
            squares[u // 2] = lax.dot_general(
                left, right, (((0,), (0,)), ((), ())), preferred_element_type=jnp.float32
            )
            weights[u // 2] = jnp.concatenate([sides[0][2], sides[1][2]], axis=0)

    def finish():
        return [force for unit in range(BATCH // 2) for force in moment_sums(squares[unit], weights[unit])]

    def add(i, sums):
        for u in range(BATCH):
            at = pl.ds(pl.multiple_of(first(i, u) * 8, 8), 8)
            acc[at, :] += sums[u]

    def step(i, carry):
        sums = finish()
        begin(i)
        add(i - 1, sums)
        return carry

    begin(0)
    lax.fori_loop(1, batches, step, 0)
    add(batches - 1, finish())


def run_list(targets, sources, total, null_row, own, pool, acc, squares, weights):
    for u in range(BATCH):
        targets[total + u] = 0
        sources[total + u] = null_row
    batches = jnp.maximum((total + BATCH - 1) // BATCH, 1)
    run_pairs(
        batches,
        lambda i, u: targets[i * BATCH + u],
        lambda i, u: sources[i * BATCH + u],
        own, pool, acc, squares, weights,
    )


def fetch_tables(packed, staging, tables, sem):
    for n, (ref, row) in enumerate(packed):
        staging[n] = ref[pl.ds(row, TABLE), :].astype(jnp.int32)
    copy = pltpu.make_async_copy(staging, tables, sem)
    copy.start()
    return copy


def append(begin, end, entry, targets, sources, total):
    def step(i, total):
        j = begin + i * CHUNK
        found = [entry(j + v) for v in range(CHUNK)]
        for v, (target, source, valid) in enumerate(found):
            targets[total] = target
            sources[total] = source
            total = total + jnp.where((j + v < end) & valid, 1, 0)
        return total

    return lax.fori_loop(0, lax.shift_right_logical(end - begin + (CHUNK - 1), CHUNK.bit_length() - 1), step, total)


def append_ghosts(tables, offsets, row0, stride, targets, sources, total, leaves, sent):
    lanes = tables.shape[2]
    bits = CODE.bit_length() - 1

    def slot(code, k):
        return ((code & (CODE - 1)) - (leaves + k * sent)) & (lanes - 1)

    for n, k in enumerate(offsets):
        at = row0 + n * stride

        def mine(j, n=n, k=k, at=at):
            code = tables[0, 0, j]
            leaf = tables[1 + n, 2, slot(code, k)]
            return lax.shift_right_logical(code, bits), at + 4 * leaf, leaf >= 0

        total = append(tables[0, 1, k], tables[0, 1, k + 1], mine, targets, sources, total)
        back = 7 - k

        def theirs(j, n=n, back=back, at=at):
            code = tables[1 + n, 0, j]
            leaf = tables[0, 2, slot(code, back)]
            return leaf, at + 4 * lax.shift_right_logical(code, bits), leaf >= 0

        total = append(tables[1 + n, 1, back], tables[1 + n, 1, back + 1], theirs, targets, sources, total)
    return total


def self_kernel(own, acc, squares, weights, *, leaves):
    acc[...] = jnp.zeros_like(acc)
    run_pairs(
        leaves // BATCH,
        lambda i, u: i * BATCH + u,
        lambda i, u: 4 * (i * BATCH + u),
        own, own, acc, squares, weights,
    )


def near_kernel(own, p1, p3, p4, p6, acc_in, acc, pool, staging, tables, targets, sources, squares, weights, sem, *, leaves, sent):
    rows = 4 * leaves
    stride = rows + TABLE
    parts = (own, p1, p3, p4, p6)
    copy = fetch_tables([(ref, rows) for ref in parts], staging, tables, sem)
    acc[...] = acc_in[...]
    for n, ref in enumerate(parts):
        pool[pl.ds(n * stride, stride), :] = ref[...]
    copy.wait()

    def both(j, n):
        code = tables[0, 0, j]
        t = lax.shift_right_logical(code, CODE.bit_length() - 1)
        u = code & (CODE - 1)
        targets[n] = t
        sources[n] = 4 * u
        targets[n + 1] = u
        sources[n + 1] = 4 * t
        return n + 2

    total = lax.fori_loop(tables[0, 1, LOCAL], tables[0, 1, LOCAL + 1], both, 0)
    total = append_ghosts(tables, (1, 3, 4, 6), stride, stride, targets, sources, total, leaves, sent)
    run_list(targets, sources, total, rows, own, pool, acc, squares, weights)


def corner_kernel(own, lower, upper, acc_in, out, acc, pool, staging, tables, targets, sources, squares, weights, sem, *, leaves, sent):
    rows = 4 * leaves
    stride = rows + TABLE
    parts = [(lower, 0), (lower, stride), (upper, 0), (upper, stride)]
    copy = fetch_tables([(own, rows)] + [(ref, row + rows) for ref, row in parts], staging, tables, sem)
    acc[...] = acc_in[...]
    pool[pl.ds(0, 2 * stride), :] = lower[...]
    pool[pl.ds(2 * stride, 2 * stride), :] = upper[...]
    copy.wait()
    total = append_ghosts(tables, (0, 5, 2, 7), 0, stride, targets, sources, 0, leaves, sent)
    run_list(targets, sources, total, rows, own, pool, acc, squares, weights)

    def part(c):
        return acc[pl.ds(c, leaves, stride=8), :] + acc[pl.ds(c + 4, leaves, stride=8), :]

    mass = own[pl.ds(3, leaves, stride=4), :]
    norm = part(3)
    for c in range(3):
        out[c, 0] = mass * (part(c) - own[pl.ds(c, leaves, stride=4), :] * norm)


def ring(size, step):
    return [(i, (i + step) % size) for i in range(size)]


def both_ways(value, axis):
    size = lax.axis_size(axis)
    lower = lax.ppermute(value, axis, ring(size, 1))
    upper = lax.ppermute(value, axis, ring(size, -1))
    return lower, upper


def local(positions, masses, occupancy, export_slots, export_count, pair_list, pair_count):
    leaves, lanes = masses.shape[1:]
    sent = export_slots.shape[1]
    slots_of_pairs = pair_list.shape[2]
    rows = 4 * leaves + TABLE
    f32 = jnp.float32
    smem = pl.BlockSpec(memory_space=pltpu.SMEM)
    packed = pl.pallas_call(
        functools.partial(pack_kernel, leaves=leaves, sent=sent, slots_of_pairs=slots_of_pairs),
        out_shape=pltpu.VMEM((rows, lanes), f32),
        in_specs=[vmem(), vmem(), vmem(), vmem(), smem, vmem(), smem],
        out_specs=vmem(),
        name="pack",
    )(positions, masses, occupancy, export_slots, export_count, pair_list, pair_count)

    pairing = [
        pltpu.VMEM((BATCH // 2, lanes, 2 * lanes), f32),
        pltpu.VMEM((BATCH // 2, 32, lanes), jnp.bfloat16),
    ]

    def lists(entries):
        return [
            pltpu.VMEM((5, TABLE, lanes), jnp.int32),
            pltpu.SMEM((5, TABLE, lanes), jnp.int32),
            pltpu.SMEM((entries + BATCH + CHUNK,), jnp.int32),
            pltpu.SMEM((entries + BATCH + CHUNK,), jnp.int32),
            *pairing,
            pltpu.SemaphoreType.DMA,
        ]

    def cost(blocks):
        return pl.CostEstimate(flops=blocks * lanes * lanes * 200, transcendentals=0, bytes_accessed=rows * lanes * 4)

    accumulator = pltpu.VMEM((8 * leaves, lanes), f32)
    lower_s, upper_s = both_ways(packed, "space")
    lower_r, upper_r = both_ways(packed, "sub")
    acc = pl.pallas_call(
        functools.partial(self_kernel, leaves=leaves),
        out_shape=accumulator,
        in_specs=[vmem()],
        out_specs=vmem(),
        scratch_shapes=pairing,
        cost_estimate=cost(leaves),
        name="self_pairs",
    )(on_chip(packed))
    corners = jnp.concatenate([lower_s, upper_s], axis=0)
    lower_c, upper_c = both_ways(corners, "sub")
    acc = pl.pallas_call(
        functools.partial(near_kernel, leaves=leaves, sent=sent),
        out_shape=accumulator,
        in_specs=[vmem()] * 6,
        out_specs=vmem(),
        scratch_shapes=[pltpu.VMEM((5 * rows, lanes), f32)] + lists(6 * slots_of_pairs),
        cost_estimate=cost(slots_of_pairs),
        name="near_pairs",
    )(*map(on_chip, (packed, lower_s, lower_r, upper_r, upper_s, acc)))
    return pl.pallas_call(
        functools.partial(corner_kernel, leaves=leaves, sent=sent),
        out_shape=jax.ShapeDtypeStruct((3, 1, leaves, lanes), f32),
        in_specs=[vmem()] * 4,
        out_specs=vmem(),
        scratch_shapes=[pltpu.VMEM((8 * leaves, lanes), f32), pltpu.VMEM((4 * rows, lanes), f32)]
        + lists(5 * slots_of_pairs),
        cost_estimate=cost(slots_of_pairs),
        name="corner_pairs",
    )(*map(on_chip, (packed, lower_c, upper_c, acc)))


def solution(mesh):
    return jax.shard_map(
        local,
        mesh=mesh,
        in_specs=(
            P(None, "space", "sub", None),
            P("space", "sub", None),
            P("space", "sub"),
            P("space", "sub"),
            P("space", "sub"),
            P(None, "space", "sub"),
            P("space", "sub"),
        ),
        out_specs=P(None, "space", "sub", None),
        check_vma=False,
    )
```

time: 34.8 us -> 34.8 us (level); the launches traced: 35.1 us -> 34.7 us
  Pallas kernels: 15.1 us -> 12.1 us
  waiting for transfers between devices: 8.81 us -> 11.4 us
    ppermute x6, waiting for transfers between devices: 8.81 us -> 11.4 us  [the longest x3 7.32 us: both_ways(): lower = lax.ppermute(value, axis, ring(size, 1))]
    pallas_call x2, Pallas kernels: 9.54 us -> 7.51 us  [the longest x1 4.14 us: local(): pl.pallas_call(functools.partial(near_kernel, leaves=leaves, sent=sent),...]
    pallas_call x1, Pallas kernels: 4.4 us -> 3.45 us  [local(): pl.pallas_call(functools.partial(corner_kernel, leaves=leaves, sent=sent)...]
  transfers between devices with their start and end apart: 6 -> 6, of which waited for: 3 -> 4; matrix products, arithmetic and copies ran while one was open for 0% -> 0% of each run, Pallas kernels for 27% -> 22%
where the time goes in v1:
time: 34.8 us; the launch traced here: 34.7 us
  Pallas kernels  12.1 us (35%)
  waiting for transfers between devices  11.4 us (33%)
  starting transfers between devices  9.83 us (28%)
  between operations  1.35 us (4%)
    ppermute x3, waiting for transfers between devices, both_ways(): lower = lax.ppermute(value, axis, ring(size, 1))  7.32 us
    ppermute x3, starting transfers between devices, both_ways(): upper = lax.ppermute(value, axis, ring(size, -1))  6.8 us
    pallas_call x1, Pallas kernels, local(): pl.pallas_call(functools.partial(near_kernel, leaves=leaves, sent=sent),...  4.14 us
    ppermute x3, waiting for transfers between devices, both_ways(): upper = lax.ppermute(value, axis, ring(size, -1))  4.06 us
    pallas_call x1, Pallas kernels, local(): pl.pallas_call(functools.partial(corner_kernel, leaves=leaves, sent=sent)...  3.45 us
    pallas_call x1, Pallas kernels, local(): pl.pallas_call(functools.partial(self_kernel, leaves=leaves), out_shape=a...  3.37 us
    ppermute x3, starting transfers between devices, both_ways(): lower = lax.ppermute(value, axis, ring(size, 1))  3.02 us
    pallas_call x1, Pallas kernels, local(): pl.pallas_call(functools.partial(pack_kernel, leaves=leaves, sent=sent, s...  1.15 us
  transfers between devices with their start and end apart: 6, of which 4 were waited for; matrix products, arithmetic and copies ran while one was open for 0% of the time, Pallas kernels for 22%

profile of v1, /device:TPU:0, one launch (start us, length us, event | category | flops | bytes accessed | tf_op | source)
XLA Modules:
  0.0 34.7 jit_solution(5231880153368819351)
XLA Ops:
  1.3 1.1 %pack.1.own = f32[264,128]{1,0:T(8,128)S(1)} custom-call(f32[3,1,64,128]{3,2,1,0:T(8,128)} %pos.1, f32[1,64,128]{2,1,0:T(8,128)} %mass.1, s32[1,64]{1,0:T(1,128)} %occupancy.1, s32[1,32]{1,0:T(1,128)} %slots.1, s32[1,1]{1,0:T(1,128)S(6)} %copy.9.count, s32[2,1,64]{2,1,0:T(1,128)} %pairs.1, s32[1,1]{1,0:T(1,128)S(6)} %copy.10.pair_count), custom_call_target="tpu_custom_call" | custom-call | tf_op jit(solution)/shard_map/pack/pallas_call | solution.py:285
  2.5 3.0 %collective-permute-start = (f32[264,128]{1,0:T(8,128)S(1)}, f32[264,128]{1,0:T(8,128)S(1)}, u32[]{:S(2)}, u32[]{:S(2)}) collective-permute-start(f32[264,128]{1,0:T(8,128)S(1)} %pack.1.own), channel_id=1, source_target_pairs={{0,8},{8,16},{16,24},{24,0},{1,9},{9,17},{17,25},{25,1},{2,10},{10... | collective-permute-start | bytes 405512 | tf_op jit(solution)/shard_map/ppermute | solution.py:273
  5.5 1.0 %collective-permute-start.1 = (f32[264,128]{1,0:T(8,128)S(1)}, f32[264,128]{1,0:T(8,128)S(1)}, u32[]{:S(2)}, u32[]{:S(2)}) collective-permute-start(f32[264,128]{1,0:T(8,128)S(1)} %pack.1.own), channel_id=1, source_target_pairs={{0,24},{8,0},{16,8},{24,16},{1,25},{9,1},{17,9},{25,17},{2,26},{10... | collective-permute-start | bytes 405512 | tf_op jit(solution)/shard_map/ppermute | solution.py:274
  6.5 4.4 %collective-permute-done.p1 = f32[264,128]{1,0:T(8,128)S(1)} collective-permute-done((f32[264,128]{1,0:T(8,128)S(1)}, f32[264,128]{1,0:T(8,128)S(1)}, u32[]{:S(2)}, u32[]{:S(2)}) %collective-permute-start) | collective-permute-done | bytes 135200 | tf_op jit(solution)/shard_map/ppermute | solution.py:273
  10.9 2.3 %collective-permute-done.1.p6 = f32[264,128]{1,0:T(8,128)S(1)} collective-permute-done((f32[264,128]{1,0:T(8,128)S(1)}, f32[264,128]{1,0:T(8,128)S(1)}, u32[]{:S(2)}, u32[]{:S(2)}) %collective-permute-start.1) | collective-permute-done | bytes 135200 | tf_op jit(solution)/shard_map/ppermute | solution.py:274
  13.2 2.2 %collective-permute-start.3 = (f32[528,128]{1,0:T(8,128)S(1)}, f32[528,128]{1,0:T(8,128)S(1)}, u32[]{:S(2)}, u32[]{:S(2)}) collective-permute-start(f32[528,128]{1,0:T(8,128)S(1)} %constant_dynamic-update-slice_fusion), channel_id=1, source_target_pairs={{0,7},{1,0},{2,1},{3,2},{4,3},{5,4},{6,5},{7,6},{8,15},{9,8},{10,9... | collective-permute-start | bytes 811016 | tf_op jit(solution)/shard_map/ppermute | solution.py:274
  15.4 0.0 collective-permute-start.2
  15.4 3.5 %collective-permute-start.5 = (f32[264,128]{1,0:T(8,128)S(1)}, f32[264,128]{1,0:T(8,128)S(1)}, u32[]{:S(2)}, u32[]{:S(2)}) collective-permute-start(f32[264,128]{1,0:T(8,128)S(1)} %pack.1.own), channel_id=1, source_target_pairs={{0,7},{1,0},{2,1},{3,2},{4,3},{5,4},{6,5},{7,6},{8,15},{9,8},{10,9... | collective-permute-start | bytes 405512 | tf_op jit(solution)/shard_map/ppermute | solution.py:274
  19.0 0.0 collective-permute-start.4
  19.0 3.4 %self_pairs.1.acc_in = f32[512,128]{1,0:T(8,128)S(1)} custom-call(f32[264,128]{1,0:T(8,128)S(1)} %pack.1.own), custom_call_target="tpu_custom_call" | custom-call | flops 209715200 | bytes 135168 | tf_op jit(solution)/shard_map/self_pairs/pallas_call | solution.py:314
  22.3 1.8 %collective-permute-done.5.p4 = f32[264,128]{1,0:T(8,128)S(1)} collective-permute-done((f32[264,128]{1,0:T(8,128)S(1)}, f32[264,128]{1,0:T(8,128)S(1)}, u32[]{:S(2)}, u32[]{:S(2)}) %collective-permute-start.5) | collective-permute-done | bytes 135200 | tf_op jit(solution)/shard_map/ppermute | solution.py:274
  24.1 3.0 %collective-permute-done.4.p3 = f32[264,128]{1,0:T(8,128)S(1)} collective-permute-done((f32[264,128]{1,0:T(8,128)S(1)}, f32[264,128]{1,0:T(8,128)S(1)}, u32[]{:S(2)}, u32[]{:S(2)}) %collective-permute-start.4) | collective-permute-done | bytes 135200 | tf_op jit(solution)/shard_map/ppermute | solution.py:273
  27.1 4.1 %near_pairs.1.acc_in = f32[512,128]{1,0:T(8,128)S(1)} custom-call(f32[264,128]{1,0:T(8,128)S(1)} %pack.1.own, f32[264,128]{1,0:T(8,128)S(1)} %collective-permute-done.p1, f32[264,128]{1,0:T(8,128)S(1)} %collective-permute-done.4.p3, f32[264,128]{1,0:T(8,128)S(1)} %collective-permute-done.5.p4, f32[264,128]{1,0:T(8,128)S(1)} %collective-permute-done.1.p6, ...), custom_call_target="tpu_custom_call" | custom-call | flops 209715200 | bytes 135168 | tf_op jit(solution)/shard_map/near_pairs/pallas_call | solution.py:325
  31.2 0.0 collective-permute-done.3.upper
  31.2 0.0 collective-permute-done.2.lower
  31.2 3.5 %corner_pairs.1 = f32[3,1,64,128]{3,2,1,0:T(8,128)} custom-call(f32[264,128]{1,0:T(8,128)S(1)} %pack.1.own, f32[528,128]{1,0:T(8,128)S(1)} %collective-permute-done.2.lower, f32[528,128]{1,0:T(8,128)S(1)} %collective-permute-done.3.upper, f32[512,128]{1,0:T(8,128)S(1)} %near_pairs.1.acc_in), custom_call_target="tpu_custom_call" | custom-call | flops 209715200 | bytes 135168 | tf_op jit(solution)/shard_map/corner_pairs/pallas_call | solution.py:334
  (2 shorter events, 0.0 us)
Async XLA Ops:
  2.5 8.4 %collective-permute-start = (f32[264,128]{1,0:T(8,128)S(1)}, f32[264,128]{1,0:T(8,128)S(1)}, u32[]{:S(2)}, u32[]{:S(2)}) collective-permute-start(f32[264,128]{1,0:T(8,128)S(1)} %pack.1.own), channel_id=1, source_target_pairs={{0,8},{8,16},{16,24},{24,0},{1,9},{9,17},{17,25},{25,1},{2,10},{10... | collective-permute-start | bytes 405512 | tf_op jit(solution)/shard_map/ppermute | solution.py:273
  5.5 7.7 %collective-permute-start.1 = (f32[264,128]{1,0:T(8,128)S(1)}, f32[264,128]{1,0:T(8,128)S(1)}, u32[]{:S(2)}, u32[]{:S(2)}) collective-permute-start(f32[264,128]{1,0:T(8,128)S(1)} %pack.1.own), channel_id=1, source_target_pairs={{0,24},{8,0},{16,8},{24,16},{1,25},{9,1},{17,9},{25,17},{2,26},{10... | collective-permute-start | bytes 405512 | tf_op jit(solution)/shard_map/ppermute | solution.py:274
  13.2 18.0 %collective-permute-start.3 = (f32[528,128]{1,0:T(8,128)S(1)}, f32[528,128]{1,0:T(8,128)S(1)}, u32[]{:S(2)}, u32[]{:S(2)}) collective-permute-start(f32[528,128]{1,0:T(8,128)S(1)} %constant_dynamic-update-slice_fusion), channel_id=1, source_target_pairs={{0,7},{1,0},{2,1},{3,2},{4,3},{5,4},{6,5},{7,6},{8,15},{9,8},{10,9... | collective-permute-start | bytes 811016 | tf_op jit(solution)/shard_map/ppermute | solution.py:274
  15.4 15.8 %collective-permute-start.2 = (f32[528,128]{1,0:T(8,128)S(1)}, f32[528,128]{1,0:T(8,128)S(1)}, u32[]{:S(2)}, u32[]{:S(2)}) collective-permute-start(f32[528,128]{1,0:T(8,128)S(1)} %constant_dynamic-update-slice_fusion), channel_id=1, source_target_pairs={{0,1},{1,2},{2,3},{3,4},{4,5},{5,6},{6,7},{7,0},{8,9},{9,10},{10,1... | collective-permute-start | bytes 811016 | tf_op jit(solution)/shard_map/ppermute | solution.py:273
  15.4 8.7 %collective-permute-start.5 = (f32[264,128]{1,0:T(8,128)S(1)}, f32[264,128]{1,0:T(8,128)S(1)}, u32[]{:S(2)}, u32[]{:S(2)}) collective-permute-start(f32[264,128]{1,0:T(8,128)S(1)} %pack.1.own), channel_id=1, source_target_pairs={{0,7},{1,0},{2,1},{3,2},{4,3},{5,4},{6,5},{7,6},{8,15},{9,8},{10,9... | collective-permute-start | bytes 405512 | tf_op jit(solution)/shard_map/ppermute | solution.py:274
  19.0 8.1 %collective-permute-start.4 = (f32[264,128]{1,0:T(8,128)S(1)}, f32[264,128]{1,0:T(8,128)S(1)}, u32[]{:S(2)}, u32[]{:S(2)}) collective-permute-start(f32[264,128]{1,0:T(8,128)S(1)} %pack.1.own), channel_id=1, source_target_pairs={{0,1},{1,2},{2,3},{3,4},{4,5},{5,6},{6,7},{7,0},{8,9},{9,10},{10,1... | collective-permute-start | bytes 405512 | tf_op jit(solution)/shard_map/ppermute | solution.py:273

commit v2 on v1

v2 whole, which is shorter than its diff:
```python
import functools

import jax
import jax.numpy as jnp
from jax import lax
from jax.experimental import pallas as pl
from jax.experimental.pallas import tpu as pltpu
from jax.sharding import PartitionSpec as P


LOCAL = 8
SOFTEN = 0.05
CENTER = 0.75
TABLE = 8
CODE = 1024
SELF_BATCH, NEAR_BATCH, FAR_BATCH = 16, 8, 12
CHUNK = 4


def vmem():
    return pl.BlockSpec(memory_space=pltpu.VMEM)


def on_chip(value):
    return pltpu.with_memory_space_constraint(value, pltpu.VMEM)


def column(row, size):
    a = lax.broadcasted_iota(jnp.int32, (size, size), 0)
    b = lax.broadcasted_iota(jnp.int32, (size, size), 1)
    return jnp.sum(jnp.where(a == b, row[:, :size], 0), axis=1, keepdims=True)


def pack_kernel(pos, mass, occupancy, slots, pairs, counts, out, *, leaves, sent, slots_of_pairs):
    lanes = mass.shape[-1]
    occ = column(occupancy[...], leaves)
    lane = lax.broadcasted_iota(jnp.int32, (leaves, lanes), 1)
    live = jnp.where(lane < occ, mass[0], 0.0)
    for c in range(3):
        out[pl.ds(c, leaves, stride=4), :] = pos[c, 0] - CENTER
    out[pl.ds(3, leaves, stride=4), :] = live
    n = slots_of_pairs
    target = pairs[0]
    source = pairs[1]
    index = lax.broadcasted_iota(jnp.int32, (1, n), 1)
    key = jnp.where(source < leaves, LOCAL, (source - leaves) // sent)
    key = jnp.where(index < counts[:, lanes // 2 : lanes // 2 + 1], key, LOCAL + 1)
    code = target * CODE + source
    order = key * CODE + index
    order_col = column(order, n)
    code_col = column(code, n)
    rank = jnp.sum((order < order_col).astype(jnp.int32), axis=1, keepdims=True)
    place = lax.broadcasted_iota(jnp.int32, (n, lanes), 1)
    sorted_code = jnp.sum(jnp.where(place == rank, code_col, 0), axis=0, keepdims=True)
    starts = jnp.sum((order_col < place * CODE).astype(jnp.int32), axis=0, keepdims=True)
    g = lax.broadcasted_iota(jnp.int32, (1, sent), 1)
    alive = jnp.where(g < counts[:, 0:1], slots[...], -1)
    base = 4 * leaves
    out[pl.ds(base, TABLE), :] = jnp.zeros((TABLE, lanes), jnp.float32)
    out[pl.ds(base, 1), :] = sorted_code.astype(jnp.float32)
    out[pl.ds(base + 1, 1), :] = starts.astype(jnp.float32)
    out[pl.ds(base + 2, 1), :sent] = alive.astype(jnp.float32)


def split3(a):
    a1 = a.astype(jnp.bfloat16).astype(jnp.float32)
    r = a - a1
    a2 = r.astype(jnp.bfloat16).astype(jnp.float32)
    return a1, a2, r - a2


STACK = 48


def target_stack(target):
    row = lax.broadcasted_iota(jnp.int32, target.shape, 0)
    xt = jnp.where(row < 3, target, 0.0)
    qt = jnp.sum(xt * xt, axis=0, keepdims=True)
    b = jnp.where(row < 3, xt, jnp.where(row == 3, 1.0, jnp.where(row == 4, qt, 0.0)))
    b1, b2, b3 = split3(b)
    return jnp.concatenate([b1, b2, b1, b2, b3, b1], axis=0).astype(jnp.bfloat16)


def source_stacks(source):
    row = lax.broadcasted_iota(jnp.int32, source.shape, 0)
    xs = jnp.where(row < 3, source, 0.0)
    ms = source[3:4]
    qs = jnp.sum(xs * xs, axis=0, keepdims=True) + SOFTEN
    a = jnp.where(row < 3, -2.0 * xs, jnp.where(row == 3, qs, jnp.where(row == 4, 1.0, 0.0)))
    g = jnp.where(row < 3, xs * ms, jnp.where(row == 3, ms, 0.0))
    a1, a2, a3 = split3(a)
    g1, g2, g3 = split3(g)
    left = jnp.concatenate([a1, a1, a2, a2, a1, a3], axis=0).astype(jnp.bfloat16)
    moments = jnp.concatenate([g1 + pltpu.roll(g2, 4, 0), g3], axis=0).astype(jnp.bfloat16)
    return left, moments


def moment_sums(softened, moments):
    lanes = softened.shape[1] // 2
    inverse = lax.rsqrt(softened)
    scaled = jnp.maximum((1.0 + SOFTEN) - softened, 0.0) * inverse
    weight = scaled * scaled * inverse
    high = weight.astype(jnp.bfloat16)
    low = (weight - high.astype(jnp.float32)).astype(jnp.bfloat16)
    total = jnp.dot(
        jnp.concatenate([moments, moments], axis=1),
        jnp.concatenate([high, low], axis=0),
        preferred_element_type=jnp.float32,
    )
    return (
        total[0:8, :lanes] + total[8:16, :lanes],
        total[16:24, lanes:] + total[24:32, lanes:],
    )


def run_pairs(batches, first, second, target_of, pool, acc, squares, weights):
    lanes = pool.shape[1]
    size = 2 * squares.shape[0]
    none = jnp.zeros((STACK, lanes), jnp.bfloat16)

    def begin(i):
        begun = []
        for u in range(0, size, 2):
            rights = [target_of(first(i, v)) for v in (u, u + 1)]
            lefts = [source_stacks(pool[pl.ds(second(i, v), 8), :]) for v in (u, u + 1)]
            left = jnp.concatenate([lefts[0][0], lefts[1][0]], axis=0)
            right = jnp.concatenate(
                [
                    jnp.concatenate([rights[0], none], axis=1),
                    jnp.concatenate([none, rights[1]], axis=1),
                ],
                axis=0,
            )
            square = lax.dot_general(left, right, (((0,), (0,)), ((), ())), preferred_element_type=jnp.float32)
            begun.append((square, jnp.concatenate([lefts[0][1], lefts[1][1]], axis=0)))
        return begun

    def keep(begun):
        for unit, (square, moments) in enumerate(begun):
            squares[unit] = square
            weights[unit] = moments

    def finish():
        return [force for unit in range(size // 2) for force in moment_sums(squares[unit], weights[unit])]

    def add(i, sums):
        for u in range(size):
            at = pl.ds(pl.multiple_of(first(i, u) * 8, 8), 8)
            acc[at, :] += sums[u]

    def step(i, carry):
        begun = begin(i)
        sums = finish()
        keep(begun)
        add(i - 1, sums)
        return carry

    keep(begin(0))
    lax.fori_loop(1, batches, step, 0)
    add(batches - 1, finish())


def run_list(targets, sources, total, null_row, stacks, pool, acc, squares, weights):
    size = 2 * squares.shape[0]
    for u in range(size):
        targets[total + u] = 0
        sources[total + u] = null_row
    batches = jnp.maximum(lax.div(total + (size - 1), size), 1)
    run_pairs(
        batches,
        lambda i, u: targets[i * size + u],
        lambda i, u: sources[i * size + u],
        lambda leaf: stacks[leaf],
        pool, acc, squares, weights,
    )


def append(begin, end, entry, targets, sources, total):
    def step(i, total):
        j = begin + i * CHUNK
        found = [entry(j + v) for v in range(CHUNK)]
        for v, (target, source, valid) in enumerate(found):
            targets[total] = target
            sources[total] = source
            total = total + jnp.where((j + v < end) & valid, 1, 0)
        return total

    return lax.fori_loop(0, lax.shift_right_logical(end - begin + (CHUNK - 1), CHUNK.bit_length() - 1), step, total)


def append_ghosts(tables, offsets, first, stride, targets, sources, total, leaves, sent):
    lanes = tables.shape[2]
    bits = CODE.bit_length() - 1

    def slot(code, k):
        return ((code & (CODE - 1)) - (leaves + k * sent)) & (lanes - 1)

    for n, k in enumerate(offsets):
        at = (first - 1 + n) * stride

        def mine(j, n=n, k=k, at=at):
            code = tables[0, 0, j]
            leaf = tables[first + n, 2, slot(code, k)]
            return lax.shift_right_logical(code, bits), at + 4 * leaf, leaf >= 0

        total = append(tables[0, 1, k], tables[0, 1, k + 1], mine, targets, sources, total)
        back = 7 - k

        def theirs(j, n=n, back=back, at=at):
            code = tables[first + n, 0, j]
            leaf = tables[0, 2, slot(code, back)]
            return leaf, at + 4 * lax.shift_right_logical(code, bits), leaf >= 0

        total = append(tables[first + n, 1, back], tables[first + n, 1, back + 1], theirs, targets, sources, total)
    return total


def self_kernel(own, acc, stacks, squares, weights, *, leaves):
    acc[...] = jnp.zeros_like(acc)
    size = 2 * squares.shape[0]

    def target_of(leaf):
        stack = target_stack(own[pl.ds(4 * leaf, 8), :])
        stacks[leaf] = stack
        return stack

    run_pairs(
        leaves // size,
        lambda i, u: i * size + u,
        lambda i, u: 4 * (i * size + u),
        target_of,
        own, acc, squares, weights,
    )


def load_parts(own, refs, pool, staging, tables, sem):
    stride = own.shape[0]
    parts = [(ref, row) for ref in refs for row in range(0, ref.shape[0], stride)]
    for n, (ref, row) in enumerate([(own, 0), *parts]):
        staging[n] = ref[pl.ds(row + stride - TABLE, TABLE), :].astype(jnp.int32)
    copy = pltpu.make_async_copy(staging, tables, sem)
    copy.start()
    for n, (ref, row) in enumerate(parts):
        pool[pl.ds(n * stride, stride), :] = ref[pl.ds(row, stride), :]
    return copy


def near_kernel(own, space_lower, space_upper, sub_a, sub_b, corner_a, stacks, acc_in, acc, pool, staging, tables, targets, sources, squares, weights, sem, *, leaves, sent, odd_of):
    rows = 4 * leaves
    stride = rows + TABLE
    odd = odd_of()
    copy = load_parts(own, (own, space_lower, space_upper, sub_a, sub_b, corner_a), pool, staging, tables, sem)
    acc[...] = acc_in[...]
    copy.wait()

    def both(j, n):
        code = tables[0, 0, j]
        t = lax.shift_right_logical(code, CODE.bit_length() - 1)
        u = code & (CODE - 1)
        targets[n] = t
        sources[n] = 4 * u
        targets[n + 1] = u
        sources[n + 1] = 4 * t
        return n + 2

    total = lax.fori_loop(tables[0, 1, LOCAL], tables[0, 1, LOCAL + 1], both, 0)
    offsets = (1, 6, 4 - odd, 3 + odd, 2 - 2 * odd, 7 - 2 * odd)
    total = append_ghosts(tables, offsets, 2, stride, targets, sources, total, leaves, sent)
    run_list(targets, sources, total, rows, stacks, pool, acc, squares, weights)


def far_kernel(own, corner_b, stacks, acc_in, out, acc, pool, staging, tables, targets, sources, squares, weights, sem, *, leaves, sent, odd_of):
    rows = 4 * leaves
    stride = rows + TABLE
    odd = odd_of()
    copy = load_parts(own, (corner_b,), pool, staging, tables, sem)
    acc[...] = acc_in[...]
    copy.wait()
    offsets = (2 * odd, 5 + 2 * odd)
    total = append_ghosts(tables, offsets, 1, stride, targets, sources, 0, leaves, sent)
    run_list(targets, sources, total, rows, stacks, pool, acc, squares, weights)

    def part(c):
        return acc[pl.ds(c, leaves, stride=8), :] + acc[pl.ds(c + 4, leaves, stride=8), :]

    mass = own[pl.ds(3, leaves, stride=4), :]
    norm = part(3)
    for c in range(3):
        out[c, 0] = mass * (part(c) - own[pl.ds(c, leaves, stride=4), :] * norm)


def ring(size, step):
    return [(i, (i + step) % size) for i in range(size)]


def both_ways(value, axis):
    size = lax.axis_size(axis)
    lower = lax.ppermute(value, axis, ring(size, 1))
    upper = lax.ppermute(value, axis, ring(size, -1))
    return lower, upper


def swaps(size, first):
    pairs = [(i, (i + 1) % size) for i in range(first, size, 2)]
    return pairs + [(j, i) for i, j in pairs]


def by_swaps(value, axis):
    size = lax.axis_size(axis)
    even = size % 2 == 0
    a = lax.ppermute(value, axis, swaps(size, 0) if even else ring(size, 1))
    b = lax.ppermute(value, axis, swaps(size, 1) if even else ring(size, -1))
    return a, b


def odd_index(axis):
    return lax.axis_index(axis) % 2 if lax.axis_size(axis) % 2 == 0 else jnp.int32(1)


def local(positions, masses, occupancy, export_slots, export_count, pair_list, pair_count):
    leaves, lanes = masses.shape[1:]
    sent = export_slots.shape[1]
    slots_of_pairs = pair_list.shape[2]
    rows = 4 * leaves + TABLE
    f32 = jnp.float32
    lane = lax.broadcasted_iota(jnp.int32, (1, lanes), 1)
    counts = jnp.where(lane < lanes // 2, export_count[0, 0], pair_count[0, 0])
    packed = pl.pallas_call(
        functools.partial(pack_kernel, leaves=leaves, sent=sent, slots_of_pairs=slots_of_pairs),
        out_shape=pltpu.VMEM((rows, lanes), f32),
        in_specs=[vmem()] * 6,
        out_specs=vmem(),
        name="pack",
    )(positions, masses, occupancy, export_slots, pair_list, on_chip(counts))

    def pairing(batch):
        return [
            pltpu.VMEM((batch // 2, lanes, 2 * lanes), f32),
            pltpu.VMEM((batch // 2, 32, lanes), jnp.bfloat16),
        ]

    def lists(parts, entries, batch):
        return [
            pltpu.VMEM((parts, TABLE, lanes), jnp.int32),
            pltpu.SMEM((parts, TABLE, lanes), jnp.int32),
            pltpu.SMEM((entries + batch + CHUNK,), jnp.int32),
            pltpu.SMEM((entries + batch + CHUNK,), jnp.int32),
            *pairing(batch),
            pltpu.SemaphoreType.DMA,
        ]

    def cost(blocks):
        return pl.CostEstimate(flops=blocks * lanes * lanes * 200, transcendentals=0, bytes_accessed=rows * lanes * 4)

    accumulator = pltpu.VMEM((8 * leaves, lanes), f32)
    sizes = dict(leaves=leaves, sent=sent, odd_of=functools.partial(odd_index, "sub"))
    space_lower, space_upper = both_ways(packed, "space")
    sub_a, sub_b = by_swaps(packed, "sub")
    acc, stacks = pl.pallas_call(
        functools.partial(self_kernel, leaves=leaves),
        out_shape=(accumulator, pltpu.VMEM((leaves, STACK, lanes), jnp.bfloat16)),
        in_specs=[vmem()],
        out_specs=(vmem(), vmem()),
        scratch_shapes=pairing(SELF_BATCH),
        cost_estimate=cost(leaves),
        name="self_pairs",
    )(on_chip(packed))
    corners = jnp.concatenate([space_lower, space_upper], axis=0)
    corner_a, corner_b = by_swaps(corners, "sub")
    acc = pl.pallas_call(
        functools.partial(near_kernel, **sizes),
        out_shape=accumulator,
        in_specs=[vmem()] * 8,
        out_specs=vmem(),
        scratch_shapes=[pltpu.VMEM((7 * rows, lanes), f32)]
        + lists(8, 8 * slots_of_pairs, NEAR_BATCH),
        cost_estimate=cost(slots_of_pairs),
        name="near_pairs",
    )(*map(on_chip, (packed, space_lower, space_upper, sub_a, sub_b, corner_a, stacks, acc)))
    return pl.pallas_call(
        functools.partial(far_kernel, **sizes),
        out_shape=jax.ShapeDtypeStruct((3, 1, leaves, lanes), f32),
        in_specs=[vmem()] * 4,
        out_specs=vmem(),
        scratch_shapes=[pltpu.VMEM((8 * leaves, lanes), f32), pltpu.VMEM((2 * rows, lanes), f32)]
        + lists(3, 3 * slots_of_pairs, FAR_BATCH),
        cost_estimate=cost(slots_of_pairs),
        name="far_pairs",
    )(*map(on_chip, (packed, corner_b, stacks, acc)))


def solution(mesh):
    return jax.shard_map(
        local,
        mesh=mesh,
        in_specs=(
            P(None, "space", "sub", None),
            P("space", "sub", None),
            P("space", "sub"),
            P("space", "sub"),
            P("space", "sub"),
            P(None, "space", "sub"),
            P("space", "sub"),
        ),
        out_specs=P(None, "space", "sub", None),
        check_vma=False,
    )
```

time: 34.8 us -> 33.7 us (0.968)
  starting transfers between devices: 9.83 us -> 7.85 us
  waiting for transfers between devices: 11.4 us -> 13.2 us
  Pallas kernels: 12.1 us -> 11.1 us
    ppermute x0 -> x4, waiting for transfers between devices: none -> 6.53 us  [the longest x2 6.53 us: by_swaps(): b = lax.ppermute(value, axis, swaps(size, 1) if even else ring(size, -1))]
    ppermute x3 -> x1, starting transfers between devices: 6.8 us -> 1.02 us  [both_ways(): upper = lax.ppermute(value, axis, ring(size, -1))]
    ppermute x0 -> x4, starting transfers between devices: none -> 3.81 us  [the longest x2 3.74 us: by_swaps(): b = lax.ppermute(value, axis, swaps(size, 1) if even else ring(size, -1))]
    ppermute x3 -> x1, waiting for transfers between devices: 7.32 us -> 4.37 us  [both_ways(): lower = lax.ppermute(value, axis, ring(size, 1))]
    ppermute x3 -> x1, waiting for transfers between devices: 4.06 us -> 2.28 us  [both_ways(): upper = lax.ppermute(value, axis, ring(size, -1))]
    pallas_call x3, Pallas kernels: 11 us -> 9.93 us  [the longest x1 4.96 us: local(): pl.pallas_call(functools.partial(near_kernel, **sizes), out_shape=accumul...]
    ppermute x3 -> x1, starting transfers between devices: 3.02 us -> 3.02 us  [both_ways(): lower = lax.ppermute(value, axis, ring(size, 1))]
  transfers between devices with their start and end apart: 6 -> 6, of which waited for: 4 -> 3; matrix products, arithmetic and copies ran while one was open for 0% -> 0% of each run, Pallas kernels for 22% -> 23%
where the time goes in v2:
time: 33.7 us; the launch traced here: 33.6 us
  waiting for transfers between devices  13.2 us (39%)
  Pallas kernels  11.1 us (33%)
  starting transfers between devices  7.85 us (23%)
  between operations  1.35 us (4%)
    ppermute x2, waiting for transfers between devices, by_swaps(): b = lax.ppermute(value, axis, swaps(size, 1) if even else ring(size, -1))  6.53 us
    pallas_call x1, Pallas kernels, local(): pl.pallas_call(functools.partial(near_kernel, **sizes), out_shape=accumul...  4.96 us
    ppermute x1, waiting for transfers between devices, both_ways(): lower = lax.ppermute(value, axis, ring(size, 1))  4.37 us
    ppermute x2, starting transfers between devices, by_swaps(): b = lax.ppermute(value, axis, swaps(size, 1) if even else ring(size, -1))  3.74 us
    ppermute x1, starting transfers between devices, both_ways(): lower = lax.ppermute(value, axis, ring(size, 1))  3.02 us
    pallas_call x1, Pallas kernels, local(): pl.pallas_call(functools.partial(self_kernel, leaves=leaves), out_shape=(...  2.62 us
    pallas_call x1, Pallas kernels, local(): pl.pallas_call(functools.partial(far_kernel, **sizes), out_shape=jax.Shap...  2.34 us
    ppermute x1, waiting for transfers between devices, both_ways(): upper = lax.ppermute(value, axis, ring(size, -1))  2.28 us
  transfers between devices with their start and end apart: 6, of which 3 were waited for; matrix products, arithmetic and copies ran while one was open for 0% of the time, Pallas kernels for 23%

profile of v2, /device:TPU:0, one launch (start us, length us, event | category | flops | bytes accessed | tf_op | source)
XLA Modules:
  0.0 33.6 jit_solution(7414519452730370720)
XLA Ops:
  1.3 1.2 %pack.1.own = f32[264,128]{1,0:T(8,128)S(1)} custom-call(f32[3,1,64,128]{3,2,1,0:T(8,128)} %pos.1, f32[1,64,128]{2,1,0:T(8,128)} %mass.1, s32[1,64]{1,0:T(1,128)} %occupancy.1, s32[1,32]{1,0:T(1,128)} %slots.1, s32[2,1,64]{2,1,0:T(1,128)} %pairs.1, s32[1,128]{1,0:T(1,128)S(1)} %compare_select_fusion.counts), custom_call_target="tpu_custom_call" | custom-call | tf_op jit(solution)/shard_map/pack/pallas_call | solution.py:328
  2.5 3.0 %collective-permute-start = (f32[264,128]{1,0:T(8,128)S(1)}, f32[264,128]{1,0:T(8,128)S(1)}, u32[]{:S(2)}, u32[]{:S(2)}) collective-permute-start(f32[264,128]{1,0:T(8,128)S(1)} %pack.1.own), channel_id=1, source_target_pairs={{0,8},{8,16},{16,24},{24,0},{1,9},{9,17},{17,25},{25,1},{2,10},{10... | collective-permute-start | bytes 405512 | tf_op jit(solution)/shard_map/ppermute | solution.py:298
  5.6 1.0 %collective-permute-start.1 = (f32[264,128]{1,0:T(8,128)S(1)}, f32[264,128]{1,0:T(8,128)S(1)}, u32[]{:S(2)}, u32[]{:S(2)}) collective-permute-start(f32[264,128]{1,0:T(8,128)S(1)} %pack.1.own), channel_id=1, source_target_pairs={{0,24},{8,0},{16,8},{24,16},{1,25},{9,1},{17,9},{25,17},{2,26},{10... | collective-permute-start | bytes 405512 | tf_op jit(solution)/shard_map/ppermute | solution.py:299
  6.6 4.4 %collective-permute-done.space_lower = f32[264,128]{1,0:T(8,128)S(1)} collective-permute-done((f32[264,128]{1,0:T(8,128)S(1)}, f32[264,128]{1,0:T(8,128)S(1)}, u32[]{:S(2)}, u32[]{:S(2)}) %collective-permute-start) | collective-permute-done | bytes 135200 | tf_op jit(solution)/shard_map/ppermute | solution.py:298
  11.0 2.3 %collective-permute-done.1.space_upper = f32[264,128]{1,0:T(8,128)S(1)} collective-permute-done((f32[264,128]{1,0:T(8,128)S(1)}, f32[264,128]{1,0:T(8,128)S(1)}, u32[]{:S(2)}, u32[]{:S(2)}) %collective-permute-start.1) | collective-permute-done | bytes 135200 | tf_op jit(solution)/shard_map/ppermute | solution.py:299
  13.3 0.1 collective-permute-start.5
  13.3 3.7 %collective-permute-start.2 = (f32[528,128]{1,0:T(8,128)S(1)}, f32[528,128]{1,0:T(8,128)S(1)}, u32[]{:S(2)}, u32[]{:S(2)}) collective-permute-start(f32[528,128]{1,0:T(8,128)S(1)} %constant_dynamic-update-slice_fusion), channel_id=1, source_target_pairs={{1,2},{3,4},{5,6},{7,0},{2,1},{4,3},{6,5},{0,7},{9,10},{11,12},{13... | collective-permute-start | bytes 811016 | tf_op jit(solution)/shard_map/ppermute | solution.py:312
  17.0 0.0 collective-permute-start.4
  17.1 0.0 collective-permute-start.3
  17.1 2.6 %self_pairs.1 = (f32[512,128]{1,0:T(8,128)S(1)}, bf16[64,48,128]{2,1,0:T(8,128)(2,1)S(1)}) custom-call(f32[264,128]{1,0:T(8,128)S(1)} %pack.1.own), custom_call_target="tpu_custom_call" | custom-call | flops 209715200 | bytes 135168 | tf_op jit(solution)/shard_map/self_pairs/pallas_call | solution.py:359
  19.7 6.5 %collective-permute-done.4.sub_b = f32[264,128]{1,0:T(8,128)S(1)} collective-permute-done((f32[264,128]{1,0:T(8,128)S(1)}, f32[264,128]{1,0:T(8,128)S(1)}, u32[]{:S(2)}, u32[]{:S(2)}) %collective-permute-start.4) | collective-permute-done | bytes 135200 | tf_op jit(solution)/shard_map/ppermute | solution.py:312
  26.2 0.0 collective-permute-done.3.sub_a
  26.2 0.0 collective-permute-done.5.corner_a
  26.2 5.0 %near_pairs.1.acc_in = f32[512,128]{1,0:T(8,128)S(1)} custom-call(f32[264,128]{1,0:T(8,128)S(1)} %pack.1.own, f32[264,128]{1,0:T(8,128)S(1)} %collective-permute-done.space_lower, f32[264,128]{1,0:T(8,128)S(1)} %collective-permute-done.1.space_upper, f32[264,128]{1,0:T(8,128)S(1)} %collective-permute-done.3.sub_a, ...), custom_call_target="tpu_custom_call" | custom-call | flops 209715200 | bytes 135168 | tf_op jit(solution)/shard_map/near_pairs/pallas_call | solution.py:370
  31.2 0.0 collective-permute-done.2.corner_b
  31.2 2.3 %far_pairs.1 = f32[3,1,64,128]{3,2,1,0:T(8,128)} custom-call(f32[264,128]{1,0:T(8,128)S(1)} %pack.1.own, f32[528,128]{1,0:T(8,128)S(1)} %collective-permute-done.2.corner_b, bf16[64,48,128]{2,1,0:T(8,128)(2,1)S(1)} %get-tuple-element.7.stacks, f32[512,128]{1,0:T(8,128)S(1)} %near_pairs.1.acc_in), custom_call_target="tpu_custom_call" | custom-call | flops 209715200 | bytes 135168 | tf_op jit(solution)/shard_map/far_pairs/pallas_call | solution.py:380
  (3 shorter events, 0.0 us)
Async XLA Ops:
  2.5 8.4 %collective-permute-start = (f32[264,128]{1,0:T(8,128)S(1)}, f32[264,128]{1,0:T(8,128)S(1)}, u32[]{:S(2)}, u32[]{:S(2)}) collective-permute-start(f32[264,128]{1,0:T(8,128)S(1)} %pack.1.own), channel_id=1, source_target_pairs={{0,8},{8,16},{16,24},{24,0},{1,9},{9,17},{17,25},{25,1},{2,10},{10... | collective-permute-start | bytes 405512 | tf_op jit(solution)/shard_map/ppermute | solution.py:298
  5.6 7.7 %collective-permute-start.1 = (f32[264,128]{1,0:T(8,128)S(1)}, f32[264,128]{1,0:T(8,128)S(1)}, u32[]{:S(2)}, u32[]{:S(2)}) collective-permute-start(f32[264,128]{1,0:T(8,128)S(1)} %pack.1.own), channel_id=1, source_target_pairs={{0,24},{8,0},{16,8},{24,16},{1,25},{9,1},{17,9},{25,17},{2,26},{10... | collective-permute-start | bytes 405512 | tf_op jit(solution)/shard_map/ppermute | solution.py:299
  13.3 13.0 %collective-permute-start.5 = (f32[528,128]{1,0:T(8,128)S(1)}, f32[528,128]{1,0:T(8,128)S(1)}, u32[]{:S(2)}, u32[]{:S(2)}) collective-permute-start(f32[528,128]{1,0:T(8,128)S(1)} %constant_dynamic-update-slice_fusion), channel_id=1, source_target_pairs={{0,1},{2,3},{4,5},{6,7},{1,0},{3,2},{5,4},{7,6},{8,9},{10,11},{12,... | collective-permute-start | bytes 811016 | tf_op jit(solution)/shard_map/ppermute | solution.py:311
  13.3 17.9 %collective-permute-start.2 = (f32[528,128]{1,0:T(8,128)S(1)}, f32[528,128]{1,0:T(8,128)S(1)}, u32[]{:S(2)}, u32[]{:S(2)}) collective-permute-start(f32[528,128]{1,0:T(8,128)S(1)} %constant_dynamic-update-slice_fusion), channel_id=1, source_target_pairs={{1,2},{3,4},{5,6},{7,0},{2,1},{4,3},{6,5},{0,7},{9,10},{11,12},{13... | collective-permute-start | bytes 811016 | tf_op jit(solution)/shard_map/ppermute | solution.py:312
  17.0 9.2 %collective-permute-start.4 = (f32[264,128]{1,0:T(8,128)S(1)}, f32[264,128]{1,0:T(8,128)S(1)}, u32[]{:S(2)}, u32[]{:S(2)}) collective-permute-start(f32[264,128]{1,0:T(8,128)S(1)} %pack.1.own), channel_id=1, source_target_pairs={{1,2},{3,4},{5,6},{7,0},{2,1},{4,3},{6,5},{0,7},{9,10},{11,12},{13... | collective-permute-start | bytes 405512 | tf_op jit(solution)/shard_map/ppermute | solution.py:312
  17.1 9.2 %collective-permute-start.3 = (f32[264,128]{1,0:T(8,128)S(1)}, f32[264,128]{1,0:T(8,128)S(1)}, u32[]{:S(2)}, u32[]{:S(2)}) collective-permute-start(f32[264,128]{1,0:T(8,128)S(1)} %pack.1.own), channel_id=1, source_target_pairs={{0,1},{2,3},{4,5},{6,7},{1,0},{3,2},{5,4},{7,6},{8,9},{10,11},{12,... | collective-permute-start | bytes 405512 | tf_op jit(solution)/shard_map/ppermute | solution.py:311

commit v3 on v2

--- a/solution.py
+++ b/solution.py
@@ -13,7 +13,7 @@
 CENTER = 0.75
 TABLE = 8
 CODE = 1024
-SELF_BATCH, NEAR_BATCH, FAR_BATCH = 16, 8, 12
+SELF_BATCH, NEAR_BATCH, SENT_BATCH = 16, 12, 8
 CHUNK = 4
 
 
@@ -160,7 +160,7 @@
     add(batches - 1, finish())
 
 
-def run_list(targets, sources, total, null_row, stacks, pool, acc, squares, weights):
+def run_list(targets, sources, total, null_row, target_of, pool, acc, squares, weights):
     size = 2 * squares.shape[0]
     for u in range(size):
         targets[total + u] = 0
@@ -170,7 +170,7 @@
         batches,
         lambda i, u: targets[i * size + u],
         lambda i, u: sources[i * size + u],
-        lambda leaf: stacks[leaf],
+        target_of,
         pool, acc, squares, weights,
     )
 
@@ -188,7 +188,7 @@
     return lax.fori_loop(0, lax.shift_right_logical(end - begin + (CHUNK - 1), CHUNK.bit_length() - 1), step, total)
 
 
-def append_ghosts(tables, offsets, first, stride, targets, sources, total, leaves, sent):
+def append_ghosts(tables, offsets, first, row, stride, targets, sources, total, leaves, sent):
     lanes = tables.shape[2]
     bits = CODE.bit_length() - 1
 
@@ -196,7 +196,7 @@
         return ((code & (CODE - 1)) - (leaves + k * sent)) & (lanes - 1)
 
     for n, k in enumerate(offsets):
-        at = (first - 1 + n) * stride
+        at = row + n * stride
 
         def mine(j, n=n, k=k, at=at):
             code = tables[0, 0, j]
@@ -233,24 +233,50 @@
     )
 
 
-def load_parts(own, refs, pool, staging, tables, sem):
-    stride = own.shape[0]
-    parts = [(ref, row) for ref in refs for row in range(0, ref.shape[0], stride)]
-    for n, (ref, row) in enumerate([(own, 0), *parts]):
-        staging[n] = ref[pl.ds(row + stride - TABLE, TABLE), :].astype(jnp.int32)
+def fetch_tables(parts, staging, tables, sem):
+    for n, (ref, row) in enumerate(parts):
+        staging[n] = ref[pl.ds(row, TABLE), :].astype(jnp.int32)
     copy = pltpu.make_async_copy(staging, tables, sem)
     copy.start()
+    return copy
+
+
+def forces(acc, packed, leaves):
+    def part(c):
+        return acc[pl.ds(c, leaves, stride=8), :] + acc[pl.ds(c + 4, leaves, stride=8), :]
+
+    mass = packed[pl.ds(3, leaves, stride=4), :]
+    norm = part(3)
+    return [mass * (part(c) - packed[pl.ds(c, leaves, stride=4), :] * norm) for c in range(3)]
+
+
+def sent_kernel(sub_b, corners, out, acc, staging, tables, targets, sources, squares, weights, sem, *, leaves, sent, index_of):
+    rows = 4 * leaves
+    stride = rows + TABLE
+    odd = lax.rem(index_of(), 2)
+    copy = fetch_tables([(sub_b, rows), (corners, rows), (corners, stride + rows)], staging, tables, sem)
+    acc[...] = jnp.zeros_like(acc)
+    copy.wait()
+    offsets = (2 - 2 * odd, 7 - 2 * odd)
+    total = append_ghosts(tables, offsets, 1, 0, stride, targets, sources, 0, leaves, sent)
+    run_list(
+        targets, sources, total, rows,
+        lambda leaf: target_stack(sub_b[pl.ds(4 * leaf, 8), :]),
+        corners, acc, squares, weights,
+    )
+    for c, force in enumerate(forces(acc, sub_b, leaves)):
+        out[c] = force
+
+
+def near_kernel(own, space_lower, space_upper, sub_a, sub_b, corner_a, stacks, acc_in, out, acc, pool, staging, tables, targets, sources, squares, weights, sem, *, leaves, sent, index_of):
+    rows = 4 * leaves
+    stride = rows + TABLE
+    odd = lax.rem(index_of(), 2)
+    parts = [(own, 0), (space_lower, 0), (space_upper, 0), (sub_a, 0), (sub_b, 0), (corner_a, 0), (corner_a, stride)]
+    copy = fetch_tables([(ref, row + rows) for ref, row in parts], staging, tables, sem)
+    acc[...] = acc_in[...]
     for n, (ref, row) in enumerate(parts):
         pool[pl.ds(n * stride, stride), :] = ref[pl.ds(row, stride), :]
-    return copy
-
-
-def near_kernel(own, space_lower, space_upper, sub_a, sub_b, corner_a, stacks, acc_in, acc, pool, staging, tables, targets, sources, squares, weights, sem, *, leaves, sent, odd_of):
-    rows = 4 * leaves
-    stride = rows + TABLE
-    odd = odd_of()
-    copy = load_parts(own, (own, space_lower, space_upper, sub_a, sub_b, corner_a), pool, staging, tables, sem)
-    acc[...] = acc_in[...]
     copy.wait()
 
     def both(j, n):
@@ -265,28 +291,10 @@
 
     total = lax.fori_loop(tables[0, 1, LOCAL], tables[0, 1, LOCAL + 1], both, 0)
     offsets = (1, 6, 4 - odd, 3 + odd, 2 - 2 * odd, 7 - 2 * odd)
-    total = append_ghosts(tables, offsets, 2, stride, targets, sources, total, leaves, sent)
-    run_list(targets, sources, total, rows, stacks, pool, acc, squares, weights)
-
-
-def far_kernel(own, corner_b, stacks, acc_in, out, acc, pool, staging, tables, targets, sources, squares, weights, sem, *, leaves, sent, odd_of):
-    rows = 4 * leaves
-    stride = rows + TABLE
-    odd = odd_of()
-    copy = load_parts(own, (corner_b,), pool, staging, tables, sem)
-    acc[...] = acc_in[...]
-    copy.wait()
-    offsets = (2 * odd, 5 + 2 * odd)
-    total = append_ghosts(tables, offsets, 1, stride, targets, sources, 0, leaves, sent)
-    run_list(targets, sources, total, rows, stacks, pool, acc, squares, weights)
-
-    def part(c):
-        return acc[pl.ds(c, leaves, stride=8), :] + acc[pl.ds(c + 4, leaves, stride=8), :]
-
-    mass = own[pl.ds(3, leaves, stride=4), :]
-    norm = part(3)
-    for c in range(3):
-        out[c, 0] = mass * (part(c) - own[pl.ds(c, leaves, stride=4), :] * norm)
+    total = append_ghosts(tables, offsets, 1, stride, stride, targets, sources, total, leaves, sent)
+    run_list(targets, sources, total, rows, lambda leaf: stacks[leaf], pool, acc, squares, weights)
+    for c, force in enumerate(forces(acc, own, leaves)):
+        out[c] = force
 
 
 def ring(size, step):
@@ -300,21 +308,10 @@
     return lower, upper
 
 
-def swaps(size, first):
+def swapped(value, axis, first):
+    size = lax.axis_size(axis)
     pairs = [(i, (i + 1) % size) for i in range(first, size, 2)]
-    return pairs + [(j, i) for i, j in pairs]
-
-
-def by_swaps(value, axis):
-    size = lax.axis_size(axis)
-    even = size % 2 == 0
-    a = lax.ppermute(value, axis, swaps(size, 0) if even else ring(size, 1))
-    b = lax.ppermute(value, axis, swaps(size, 1) if even else ring(size, -1))
-    return a, b
-
-
-def odd_index(axis):
-    return lax.axis_index(axis) % 2 if lax.axis_size(axis) % 2 == 0 else jnp.int32(1)
+    return lax.ppermute(value, axis, pairs + [(j, i) for i, j in pairs])
 
 
 def local(positions, masses, occupancy, export_slots, export_count, pair_list, pair_count):
@@ -353,9 +350,11 @@
         return pl.CostEstimate(flops=blocks * lanes * lanes * 200, transcendentals=0, bytes_accessed=rows * lanes * 4)
 
     accumulator = pltpu.VMEM((8 * leaves, lanes), f32)
-    sizes = dict(leaves=leaves, sent=sent, odd_of=functools.partial(odd_index, "sub"))
+    force = pltpu.VMEM((3, leaves, lanes), f32)
+    sizes = dict(leaves=leaves, sent=sent, index_of=functools.partial(lax.axis_index, "sub"))
     space_lower, space_upper = both_ways(packed, "space")
-    sub_a, sub_b = by_swaps(packed, "sub")
+    sub_a = swapped(packed, "sub", 0)
+    sub_b = swapped(packed, "sub", 1)
     acc, stacks = pl.pallas_call(
         functools.partial(self_kernel, leaves=leaves),
         out_shape=(accumulator, pltpu.VMEM((leaves, STACK, lanes), jnp.bfloat16)),
@@ -366,27 +365,28 @@
         name="self_pairs",
     )(on_chip(packed))
     corners = jnp.concatenate([space_lower, space_upper], axis=0)
-    corner_a, corner_b = by_swaps(corners, "sub")
-    acc = pl.pallas_call(
+    corner_a = swapped(corners, "sub", 0)
+    for_b = pl.pallas_call(
+        functools.partial(sent_kernel, **sizes),
+        out_shape=force,
+        in_specs=[vmem()] * 2,
+        out_specs=vmem(),
+        scratch_shapes=[pltpu.VMEM((8 * leaves, lanes), f32)] + lists(3, 3 * slots_of_pairs, SENT_BATCH),
+        cost_estimate=cost(slots_of_pairs),
+        name="sent_pairs",
+    )(*map(on_chip, (sub_b, corners)))
+    from_b = swapped(for_b, "sub", 1)
+    near = pl.pallas_call(
         functools.partial(near_kernel, **sizes),
-        out_shape=accumulator,
+        out_shape=force,
         in_specs=[vmem()] * 8,
         out_specs=vmem(),
-        scratch_shapes=[pltpu.VMEM((7 * rows, lanes), f32)]
-        + lists(8, 8 * slots_of_pairs, NEAR_BATCH),
+        scratch_shapes=[pltpu.VMEM((8 * leaves, lanes), f32), pltpu.VMEM((7 * rows, lanes), f32)]
+        + lists(7, 8 * slots_of_pairs, NEAR_BATCH),
         cost_estimate=cost(slots_of_pairs),
         name="near_pairs",
     )(*map(on_chip, (packed, space_lower, space_upper, sub_a, sub_b, corner_a, stacks, acc)))
-    return pl.pallas_call(
-        functools.partial(far_kernel, **sizes),
-        out_shape=jax.ShapeDtypeStruct((3, 1, leaves, lanes), f32),
-        in_specs=[vmem()] * 4,
-        out_specs=vmem(),
-        scratch_shapes=[pltpu.VMEM((8 * leaves, lanes), f32), pltpu.VMEM((2 * rows, lanes), f32)]
-        + lists(3, 3 * slots_of_pairs, FAR_BATCH),
-        cost_estimate=cost(slots_of_pairs),
-        name="far_pairs",
-    )(*map(on_chip, (packed, corner_b, stacks, acc)))
+    return (near + from_b)[:, None]
 
 
 def solution(mesh):

time: 33.7 us -> 32.9 us (0.976)
  waiting for transfers between devices: 13.2 us -> 10.1 us
  starting transfers between devices: 7.85 us -> 10.7 us
  Pallas kernels: 11.1 us -> 9.92 us
  other arithmetic: 0.01 us -> 0.66 us
    ppermute x4, waiting for transfers between devices: 6.53 us -> 3.4 us  [swapped(): return lax.ppermute(value, axis, pairs + [(j, i) for i, j in pairs])]
    ppermute x4, starting transfers between devices: 3.81 us -> 6.67 us  [swapped(): return lax.ppermute(value, axis, pairs + [(j, i) for i, j in pairs])]
    pallas_call x2, Pallas kernels: 7.31 us -> 6.08 us  [the longest x1 4.47 us: local(): pl.pallas_call(functools.partial(near_kernel, **sizes), out_shape=force,...]
    broadcast_in_dim x0 -> x1, other arithmetic: none -> 0.66 us  [local(): return (near + from_b)[:, None]]
  transfers between devices with their start and end apart: 6 -> 6, of which waited for: 3 -> 3; matrix products, arithmetic and copies ran while one was open for 0% -> 0% of each run, Pallas kernels for 23% -> 27%
where the time goes in v3:
time: 32.9 us; the launch traced here: 32.7 us
  starting transfers between devices  10.7 us (33%)
  waiting for transfers between devices  10.1 us (31%)
  Pallas kernels  9.92 us (30%)
  between operations  1.37 us (4%)
  other arithmetic  0.66 us (2%)
    ppermute x4, starting transfers between devices, swapped(): return lax.ppermute(value, axis, pairs + [(j, i) for i, j in pairs])  6.67 us
    pallas_call x1, Pallas kernels, local(): pl.pallas_call(functools.partial(near_kernel, **sizes), out_shape=force,...  4.47 us
    ppermute x1, waiting for transfers between devices, both_ways(): lower = lax.ppermute(value, axis, ring(size, 1))  4.37 us
    ppermute x4, waiting for transfers between devices, swapped(): return lax.ppermute(value, axis, pairs + [(j, i) for i, j in pairs])  3.4 us
    ppermute x1, starting transfers between devices, both_ways(): lower = lax.ppermute(value, axis, ring(size, 1))  3.02 us
    pallas_call x1, Pallas kernels, local(): pl.pallas_call(functools.partial(self_kernel, leaves=leaves), out_shape=(...  2.63 us
    ppermute x1, waiting for transfers between devices, both_ways(): upper = lax.ppermute(value, axis, ring(size, -1))  2.28 us
    pallas_call x1, Pallas kernels, local(): pl.pallas_call(functools.partial(sent_kernel, **sizes), out_shape=force,...  1.61 us
  transfers between devices with their start and end apart: 6, of which 3 were waited for; matrix products, arithmetic and copies ran while one was open for 0% of the time, Pallas kernels for 27%

profile of v3, /device:TPU:0, one launch (start us, length us, event | category | flops | bytes accessed | tf_op | source)
XLA Modules:
  0.0 32.7 jit_solution(10890968751838518463)
XLA Ops:
  1.3 1.2 %pack.1.own = f32[264,128]{1,0:T(8,128)S(1)} custom-call(f32[3,1,64,128]{3,2,1,0:T(8,128)} %pos.1, f32[1,64,128]{2,1,0:T(8,128)} %mass.1, s32[1,64]{1,0:T(1,128)} %occupancy.1, s32[1,32]{1,0:T(1,128)} %slots.1, s32[2,1,64]{2,1,0:T(1,128)} %pairs.1, s32[1,128]{1,0:T(1,128)S(1)} %compare_select_fusion.counts), custom_call_target="tpu_custom_call" | custom-call | tf_op jit(solution)/shard_map/pack/pallas_call | solution.py:325
  2.5 3.0 %collective-permute-start = (f32[264,128]{1,0:T(8,128)S(1)}, f32[264,128]{1,0:T(8,128)S(1)}, u32[]{:S(2)}, u32[]{:S(2)}) collective-permute-start(f32[264,128]{1,0:T(8,128)S(1)} %pack.1.own), channel_id=1, source_target_pairs={{0,8},{8,16},{16,24},{24,0},{1,9},{9,17},{17,25},{25,1},{2,10},{10... | collective-permute-start | bytes 405512 | tf_op jit(solution)/shard_map/ppermute | solution.py:306
  5.6 1.0 %collective-permute-start.1 = (f32[264,128]{1,0:T(8,128)S(1)}, f32[264,128]{1,0:T(8,128)S(1)}, u32[]{:S(2)}, u32[]{:S(2)}) collective-permute-start(f32[264,128]{1,0:T(8,128)S(1)} %pack.1.own), channel_id=1, source_target_pairs={{0,24},{8,0},{16,8},{24,16},{1,25},{9,1},{17,9},{25,17},{2,26},{10... | collective-permute-start | bytes 405512 | tf_op jit(solution)/shard_map/ppermute | solution.py:307
  6.6 4.4 %collective-permute-done.space_lower = f32[264,128]{1,0:T(8,128)S(1)} collective-permute-done((f32[264,128]{1,0:T(8,128)S(1)}, f32[264,128]{1,0:T(8,128)S(1)}, u32[]{:S(2)}, u32[]{:S(2)}) %collective-permute-start) | collective-permute-done | bytes 135200 | tf_op jit(solution)/shard_map/ppermute | solution.py:306
  11.0 2.3 %collective-permute-done.1.space_upper = f32[264,128]{1,0:T(8,128)S(1)} collective-permute-done((f32[264,128]{1,0:T(8,128)S(1)}, f32[264,128]{1,0:T(8,128)S(1)}, u32[]{:S(2)}, u32[]{:S(2)}) %collective-permute-start.1) | collective-permute-done | bytes 135200 | tf_op jit(solution)/shard_map/ppermute | solution.py:307
  13.3 0.1 collective-permute-start.4
  13.3 3.7 %collective-permute-start.3 = (f32[264,128]{1,0:T(8,128)S(1)}, f32[264,128]{1,0:T(8,128)S(1)}, u32[]{:S(2)}, u32[]{:S(2)}) collective-permute-start(f32[264,128]{1,0:T(8,128)S(1)} %pack.1.own), channel_id=1, source_target_pairs={{1,2},{3,4},{5,6},{7,0},{2,1},{4,3},{6,5},{0,7},{9,10},{11,12},{13... | collective-permute-start | bytes 405512 | tf_op jit(solution)/shard_map/ppermute | solution.py:314
  17.0 0.0 collective-permute-start.2
  17.0 3.4 %collective-permute-done.3.sub_b = f32[264,128]{1,0:T(8,128)S(1)} collective-permute-done((f32[264,128]{1,0:T(8,128)S(1)}, f32[264,128]{1,0:T(8,128)S(1)}, u32[]{:S(2)}, u32[]{:S(2)}) %collective-permute-start.3) | collective-permute-done | bytes 135200 | tf_op jit(solution)/shard_map/ppermute | solution.py:314
  20.4 1.6 %sent_pairs.1 = f32[3,64,128]{2,1,0:T(8,128)S(1)} custom-call(f32[264,128]{1,0:T(8,128)S(1)} %collective-permute-done.3.sub_b, f32[528,128]{1,0:T(8,128)S(1)} %constant_dynamic-update-slice_fusion.corners), custom_call_target="tpu_custom_call" | custom-call | flops 209715200 | bytes 135168 | tf_op jit(solution)/shard_map/sent_pairs/pallas_call | solution.py:369
  22.0 2.9 %collective-permute-start.5 = (f32[3,64,128]{2,1,0:T(8,128)S(1)}, f32[3,64,128]{2,1,0:T(8,128)S(1)}, u32[]{:S(2)}, u32[]{:S(2)}) collective-permute-start(f32[3,64,128]{2,1,0:T(8,128)S(1)} %sent_pairs.1), channel_id=1, source_target_pairs={{1,2},{3,4},{5,6},{7,0},{2,1},{4,3},{6,5},{0,7},{9,10},{11,12},{13... | collective-permute-start | bytes 294920 | tf_op jit(solution)/shard_map/ppermute | solution.py:314
  24.9 2.6 %self_pairs.1 = (f32[512,128]{1,0:T(8,128)S(1)}, bf16[64,48,128]{2,1,0:T(8,128)(2,1)S(1)}) custom-call(f32[264,128]{1,0:T(8,128)S(1)} %pack.1.own), custom_call_target="tpu_custom_call" | custom-call | flops 209715200 | bytes 135168 | tf_op jit(solution)/shard_map/self_pairs/pallas_call | solution.py:358
  27.6 0.0 collective-permute-done.2.sub_a
  27.6 0.0 collective-permute-done.4.corner_a
  27.6 4.5 %near_pairs.1 = f32[3,64,128]{2,1,0:T(8,128)S(1)} custom-call(f32[264,128]{1,0:T(8,128)S(1)} %pack.1.own, f32[264,128]{1,0:T(8,128)S(1)} %collective-permute-done.space_lower, f32[264,128]{1,0:T(8,128)S(1)} %collective-permute-done.1.space_upper, f32[264,128]{1,0:T(8,128)S(1)} %collective-permute-done.2.sub_a, f32[264,128]{1,0:T(8,128)S(1)} %collective-permute-done.3.sub_b, ...), custom_call_target="tpu_custom_call" | custom-call | flops 209715200 | bytes 135168 | tf_op jit(solution)/shard_map/near_pairs/pallas_call | solution.py:379
  32.1 0.0 collective-permute-done.5
  32.1 0.7 %add_bitcast_fusion = f32[3,1,64,128]{3,2,1,0:T(8,128)} fusion(f32[3,64,128]{2,1,0:T(8,128)S(1)} %near_pairs.1, f32[3,64,128]{2,1,0:T(8,128)S(1)} %collective-permute-done.5), kind=kLoop, calls=%fused_computation | loop fusion | flops 24576 | bytes 294912 | tf_op jit(solution)/shard_map/broadcast_in_dim | solution.py:389
  (3 shorter events, 0.0 us)
Async XLA Ops:
  2.5 8.4 %collective-permute-start = (f32[264,128]{1,0:T(8,128)S(1)}, f32[264,128]{1,0:T(8,128)S(1)}, u32[]{:S(2)}, u32[]{:S(2)}) collective-permute-start(f32[264,128]{1,0:T(8,128)S(1)} %pack.1.own), channel_id=1, source_target_pairs={{0,8},{8,16},{16,24},{24,0},{1,9},{9,17},{17,25},{25,1},{2,10},{10... | collective-permute-start | bytes 405512 | tf_op jit(solution)/shard_map/ppermute | solution.py:306
  5.6 7.7 %collective-permute-start.1 = (f32[264,128]{1,0:T(8,128)S(1)}, f32[264,128]{1,0:T(8,128)S(1)}, u32[]{:S(2)}, u32[]{:S(2)}) collective-permute-start(f32[264,128]{1,0:T(8,128)S(1)} %pack.1.own), channel_id=1, source_target_pairs={{0,24},{8,0},{16,8},{24,16},{1,25},{9,1},{17,9},{25,17},{2,26},{10... | collective-permute-start | bytes 405512 | tf_op jit(solution)/shard_map/ppermute | solution.py:307
  13.3 14.3 %collective-permute-start.4 = (f32[528,128]{1,0:T(8,128)S(1)}, f32[528,128]{1,0:T(8,128)S(1)}, u32[]{:S(2)}, u32[]{:S(2)}) collective-permute-start(f32[528,128]{1,0:T(8,128)S(1)} %constant_dynamic-update-slice_fusion.corners), channel_id=1, source_target_pairs={{0,1},{2,3},{4,5},{6,7},{1,0},{3,2},{5,4},{7,6},{8,9},{10,11},{12,... | collective-permute-start | bytes 811016 | tf_op jit(solution)/shard_map/ppermute | solution.py:314
  13.3 7.1 %collective-permute-start.3 = (f32[264,128]{1,0:T(8,128)S(1)}, f32[264,128]{1,0:T(8,128)S(1)}, u32[]{:S(2)}, u32[]{:S(2)}) collective-permute-start(f32[264,128]{1,0:T(8,128)S(1)} %pack.1.own), channel_id=1, source_target_pairs={{1,2},{3,4},{5,6},{7,0},{2,1},{4,3},{6,5},{0,7},{9,10},{11,12},{13... | collective-permute-start | bytes 405512 | tf_op jit(solution)/shard_map/ppermute | solution.py:314
  17.0 10.5 %collective-permute-start.2 = (f32[264,128]{1,0:T(8,128)S(1)}, f32[264,128]{1,0:T(8,128)S(1)}, u32[]{:S(2)}, u32[]{:S(2)}) collective-permute-start(f32[264,128]{1,0:T(8,128)S(1)} %pack.1.own), channel_id=1, source_target_pairs={{0,1},{2,3},{4,5},{6,7},{1,0},{3,2},{5,4},{7,6},{8,9},{10,11},{12,... | collective-permute-start | bytes 405512 | tf_op jit(solution)/shard_map/ppermute | solution.py:314
  22.0 10.0 %collective-permute-start.5 = (f32[3,64,128]{2,1,0:T(8,128)S(1)}, f32[3,64,128]{2,1,0:T(8,128)S(1)}, u32[]{:S(2)}, u32[]{:S(2)}) collective-permute-start(f32[3,64,128]{2,1,0:T(8,128)S(1)} %sent_pairs.1), channel_id=1, source_target_pairs={{1,2},{3,4},{5,6},{7,0},{2,1},{4,3},{6,5},{0,7},{9,10},{11,12},{13... | collective-permute-start | bytes 294920 | tf_op jit(solution)/shard_map/ppermute | solution.py:314

commit v4 on v3

--- a/solution.py
+++ b/solution.py
@@ -13,7 +13,7 @@
 CENTER = 0.75
 TABLE = 8
 CODE = 1024
-SELF_BATCH, NEAR_BATCH, SENT_BATCH = 16, 12, 8
+SELF_BATCH, NEAR_BATCH, SENT_BATCH = 16, 8, 8
 CHUNK = 4
 
 
@@ -52,14 +52,22 @@
     rank = jnp.sum((order < order_col).astype(jnp.int32), axis=1, keepdims=True)
     place = lax.broadcasted_iota(jnp.int32, (n, lanes), 1)
     sorted_code = jnp.sum(jnp.where(place == rank, code_col, 0), axis=0, keepdims=True)
-    starts = jnp.sum((order_col < place * CODE).astype(jnp.int32), axis=0, keepdims=True)
+    at_slots, at_starts = table_places(n, sent)
+    key_place = place - at_starts
+    starts = jnp.sum(((order_col < key_place * CODE) & (key_place > 0)).astype(jnp.int32), axis=0, keepdims=True)
     g = lax.broadcasted_iota(jnp.int32, (1, sent), 1)
-    alive = jnp.where(g < counts[:, 0:1], slots[...], -1)
+    alive = column(jnp.where(g < counts[:, 0:1], slots[...], -1), sent)
+    slot_place = lax.broadcasted_iota(jnp.int32, (sent, lanes), 1) - at_slots
+    slot = lax.broadcasted_iota(jnp.int32, (sent, lanes), 0)
+    table = sorted_code + starts + jnp.sum(jnp.where(slot_place == slot, alive, 0), axis=0, keepdims=True)
     base = 4 * leaves
     out[pl.ds(base, TABLE), :] = jnp.zeros((TABLE, lanes), jnp.float32)
-    out[pl.ds(base, 1), :] = sorted_code.astype(jnp.float32)
-    out[pl.ds(base + 1, 1), :] = starts.astype(jnp.float32)
-    out[pl.ds(base + 2, 1), :sent] = alive.astype(jnp.float32)
+    out[pl.ds(base, 1), :] = table.astype(jnp.float32)
+
+
+def table_places(pairs, sent):
+    at_slots = pairs
+    return at_slots, at_slots + (1 << (sent - 1).bit_length())
 
 
 def split3(a):
@@ -95,17 +103,19 @@
     return left, moments
 
 
-def moment_sums(softened, moments):
-    lanes = softened.shape[1] // 2
+def factors(softened):
     inverse = lax.rsqrt(softened)
     scaled = jnp.maximum((1.0 + SOFTEN) - softened, 0.0) * inverse
     weight = scaled * scaled * inverse
     high = weight.astype(jnp.bfloat16)
     low = (weight - high.astype(jnp.float32)).astype(jnp.bfloat16)
+    return jnp.concatenate([high, low], axis=0)
+
+
+def moment_sums(factor, moments):
+    lanes = factor.shape[1] // 2
     total = jnp.dot(
-        jnp.concatenate([moments, moments], axis=1),
-        jnp.concatenate([high, low], axis=0),
-        preferred_element_type=jnp.float32,
+        jnp.concatenate([moments, moments], axis=1), factor, preferred_element_type=jnp.float32
     )
     return (
         total[0:8, :lanes] + total[8:16, :lanes],
@@ -113,9 +123,10 @@
     )
 
 
-def run_pairs(batches, first, second, target_of, pool, acc, squares, weights):
+def run_pairs(batches, first, second, target_of, pool, acc, squares, weights, *later):
     lanes = pool.shape[1]
-    size = 2 * squares.shape[0]
+    units = range(squares.shape[0])
+    size = 2 * len(units)
     none = jnp.zeros((STACK, lanes), jnp.bfloat16)
 
     def begin(i):
@@ -140,8 +151,19 @@
             squares[unit] = square
             weights[unit] = moments
 
-    def finish():
-        return [force for unit in range(size // 2) for force in moment_sums(squares[unit], weights[unit])]
+    def middle():
+        return [(factors(squares[unit]), weights[unit]) for unit in units]
+
+    def keep_middle(made):
+        for unit, (factor, moments) in enumerate(made):
+            later[0][unit] = factor
+            later[1][unit] = moments
+
+    def finish(made):
+        return [force for factor, moments in made for force in moment_sums(factor, moments)]
+
+    def last():
+        return finish([(later[0][unit], later[1][unit]) for unit in units])
 
     def add(i, sums):
         for u in range(size):
@@ -150,28 +172,50 @@
 
     def step(i, carry):
         begun = begin(i)
-        sums = finish()
+        sums = finish(middle())
         keep(begun)
         add(i - 1, sums)
         return carry
 
+    def deep_step(i, carry):
+        begun = begin(i)
+        sums = last()
+        made = middle()
+        keep_middle(made)
+        keep(begun)
+        add(i - 2, sums)
+        return carry
+
     keep(begin(0))
-    lax.fori_loop(1, batches, step, 0)
-    add(batches - 1, finish())
-
-
-def run_list(targets, sources, total, null_row, target_of, pool, acc, squares, weights):
+    if not later:
+        lax.fori_loop(1, batches, step, 0)
+        add(batches - 1, finish(middle()))
+        return
+    begun = begin(1)
+    made = middle()
+    keep_middle(made)
+    keep(begun)
+    lax.fori_loop(2, batches, deep_step, 0)
+    sums = last()
+    made = middle()
+    keep_middle(made)
+    add(batches - 2, sums)
+    add(batches - 1, last())
+
+
+def run_list(targets, sources, total, null_row, target_of, pool, acc, squares, weights, *later):
     size = 2 * squares.shape[0]
-    for u in range(size):
+    least = 2 if later else 1
+    for u in range(least * size):
         targets[total + u] = 0
         sources[total + u] = null_row
-    batches = jnp.maximum(lax.div(total + (size - 1), size), 1)
+    batches = jnp.maximum(lax.div(total + (size - 1), size), least)
     run_pairs(
         batches,
         lambda i, u: targets[i * size + u],
         lambda i, u: sources[i * size + u],
         target_of,
-        pool, acc, squares, weights,
+        pool, acc, squares, weights, *later,
     )
 
 
@@ -188,34 +232,34 @@
     return lax.fori_loop(0, lax.shift_right_logical(end - begin + (CHUNK - 1), CHUNK.bit_length() - 1), step, total)
 
 
-def append_ghosts(tables, offsets, first, row, stride, targets, sources, total, leaves, sent):
-    lanes = tables.shape[2]
+def append_ghosts(tables, offsets, first, row, stride, targets, sources, total, leaves, sent, pairs):
+    at_slots, at_starts = table_places(pairs, sent)
     bits = CODE.bit_length() - 1
 
     def slot(code, k):
-        return ((code & (CODE - 1)) - (leaves + k * sent)) & (lanes - 1)
+        return at_slots + (((code & (CODE - 1)) - (leaves + k * sent)) & (at_starts - at_slots - 1))
 
     for n, k in enumerate(offsets):
         at = row + n * stride
 
         def mine(j, n=n, k=k, at=at):
-            code = tables[0, 0, j]
-            leaf = tables[first + n, 2, slot(code, k)]
+            code = tables[0, j]
+            leaf = tables[first + n, slot(code, k)]
             return lax.shift_right_logical(code, bits), at + 4 * leaf, leaf >= 0
 
-        total = append(tables[0, 1, k], tables[0, 1, k + 1], mine, targets, sources, total)
+        total = append(tables[0, at_starts + k], tables[0, at_starts + k + 1], mine, targets, sources, total)
         back = 7 - k
 
         def theirs(j, n=n, back=back, at=at):
-            code = tables[first + n, 0, j]
-            leaf = tables[0, 2, slot(code, back)]
+            code = tables[first + n, j]
+            leaf = tables[0, slot(code, back)]
             return leaf, at + 4 * lax.shift_right_logical(code, bits), leaf >= 0
 
-        total = append(tables[first + n, 1, back], tables[first + n, 1, back + 1], theirs, targets, sources, total)
+        total = append(tables[first + n, at_starts + back], tables[first + n, at_starts + back + 1], theirs, targets, sources, total)
     return total
 
 
-def self_kernel(own, acc, stacks, squares, weights, *, leaves):
+def self_kernel(own, acc, stacks, squares, weights, factor, moments, *, leaves):
     acc[...] = jnp.zeros_like(acc)
     size = 2 * squares.shape[0]
 
@@ -229,13 +273,13 @@
         lambda i, u: i * size + u,
         lambda i, u: 4 * (i * size + u),
         target_of,
-        own, acc, squares, weights,
+        own, acc, squares, weights, factor, moments,
     )
 
 
 def fetch_tables(parts, staging, tables, sem):
     for n, (ref, row) in enumerate(parts):
-        staging[n] = ref[pl.ds(row, TABLE), :].astype(jnp.int32)
+        staging[pl.ds(n, 1), :] = ref[pl.ds(row, 1), :].astype(jnp.int32)
     copy = pltpu.make_async_copy(staging, tables, sem)
     copy.start()
     return copy
@@ -250,7 +294,7 @@
     return [mass * (part(c) - packed[pl.ds(c, leaves, stride=4), :] * norm) for c in range(3)]
 
 
-def sent_kernel(sub_b, corners, out, acc, staging, tables, targets, sources, squares, weights, sem, *, leaves, sent, index_of):
+def sent_kernel(sub_b, corners, out, acc, staging, tables, targets, sources, squares, weights, sem, *, leaves, sent, pairs, index_of):
     rows = 4 * leaves
     stride = rows + TABLE
     odd = lax.rem(index_of(), 2)
@@ -258,7 +302,7 @@
     acc[...] = jnp.zeros_like(acc)
     copy.wait()
     offsets = (2 - 2 * odd, 7 - 2 * odd)
-    total = append_ghosts(tables, offsets, 1, 0, stride, targets, sources, 0, leaves, sent)
+    total = append_ghosts(tables, offsets, 1, 0, stride, targets, sources, 0, leaves, sent, pairs)
     run_list(
         targets, sources, total, rows,
         lambda leaf: target_stack(sub_b[pl.ds(4 * leaf, 8), :]),
@@ -268,7 +312,7 @@
         out[c] = force
 
 
-def near_kernel(own, space_lower, space_upper, sub_a, sub_b, corner_a, stacks, acc_in, out, acc, pool, staging, tables, targets, sources, squares, weights, sem, *, leaves, sent, index_of):
+def near_kernel(own, space_lower, space_upper, sub_a, sub_b, corner_a, stacks, acc_in, out, acc, pool, staging, tables, targets, sources, squares, weights, factor, moments, sem, *, leaves, sent, pairs, index_of):
     rows = 4 * leaves
     stride = rows + TABLE
     odd = lax.rem(index_of(), 2)
@@ -279,8 +323,10 @@
         pool[pl.ds(n * stride, stride), :] = ref[pl.ds(row, stride), :]
     copy.wait()
 
+    at_starts = table_places(pairs, sent)[1]
+
     def both(j, n):
-        code = tables[0, 0, j]
+        code = tables[0, j]
         t = lax.shift_right_logical(code, CODE.bit_length() - 1)
         u = code & (CODE - 1)
         targets[n] = t
@@ -289,10 +335,10 @@
         sources[n + 1] = 4 * t
         return n + 2
 
-    total = lax.fori_loop(tables[0, 1, LOCAL], tables[0, 1, LOCAL + 1], both, 0)
+    total = lax.fori_loop(tables[0, at_starts + LOCAL], tables[0, at_starts + LOCAL + 1], both, 0)
     offsets = (1, 6, 4 - odd, 3 + odd, 2 - 2 * odd, 7 - 2 * odd)
-    total = append_ghosts(tables, offsets, 1, stride, stride, targets, sources, total, leaves, sent)
-    run_list(targets, sources, total, rows, lambda leaf: stacks[leaf], pool, acc, squares, weights)
+    total = append_ghosts(tables, offsets, 1, stride, stride, targets, sources, total, leaves, sent, pairs)
+    run_list(targets, sources, total, rows, lambda leaf: stacks[leaf], pool, acc, squares, weights, factor, moments)
     for c, force in enumerate(forces(acc, own, leaves)):
         out[c] = force
 
@@ -330,19 +376,25 @@
         name="pack",
     )(positions, masses, occupancy, export_slots, pair_list, on_chip(counts))
 
-    def pairing(batch):
-        return [
+    def pairing(batch, deep):
+        stages = [
             pltpu.VMEM((batch // 2, lanes, 2 * lanes), f32),
             pltpu.VMEM((batch // 2, 32, lanes), jnp.bfloat16),
         ]
-
-    def lists(parts, entries, batch):
+        if deep:
+            stages += [
+                pltpu.VMEM((batch // 2, 2 * lanes, 2 * lanes), jnp.bfloat16),
+                pltpu.VMEM((batch // 2, 32, lanes), jnp.bfloat16),
+            ]
+        return stages
+
+    def lists(parts, entries, batch, deep):
         return [
-            pltpu.VMEM((parts, TABLE, lanes), jnp.int32),
-            pltpu.SMEM((parts, TABLE, lanes), jnp.int32),
-            pltpu.SMEM((entries + batch + CHUNK,), jnp.int32),
-            pltpu.SMEM((entries + batch + CHUNK,), jnp.int32),
-            *pairing(batch),
+            pltpu.VMEM((parts, lanes), jnp.int32),
+            pltpu.SMEM((parts, lanes), jnp.int32),
+            pltpu.SMEM((entries + 2 * batch + CHUNK,), jnp.int32),
+            pltpu.SMEM((entries + 2 * batch + CHUNK,), jnp.int32),
+            *pairing(batch, deep),
             pltpu.SemaphoreType.DMA,
         ]
 
@@ -351,7 +403,7 @@
 
     accumulator = pltpu.VMEM((8 * leaves, lanes), f32)
     force = pltpu.VMEM((3, leaves, lanes), f32)
-    sizes = dict(leaves=leaves, sent=sent, index_of=functools.partial(lax.axis_index, "sub"))
+    sizes = dict(leaves=leaves, sent=sent, pairs=slots_of_pairs, index_of=functools.partial(lax.axis_index, "sub"))
     space_lower, space_upper = both_ways(packed, "space")
     sub_a = swapped(packed, "sub", 0)
     sub_b = swapped(packed, "sub", 1)
@@ -360,7 +412,7 @@
         out_shape=(accumulator, pltpu.VMEM((leaves, STACK, lanes), jnp.bfloat16)),
         in_specs=[vmem()],
         out_specs=(vmem(), vmem()),
-        scratch_shapes=pairing(SELF_BATCH),
+        scratch_shapes=pairing(SELF_BATCH, True),
         cost_estimate=cost(leaves),
         name="self_pairs",
     )(on_chip(packed))
@@ -371,7 +423,7 @@
         out_shape=force,
         in_specs=[vmem()] * 2,
         out_specs=vmem(),
-        scratch_shapes=[pltpu.VMEM((8 * leaves, lanes), f32)] + lists(3, 3 * slots_of_pairs, SENT_BATCH),
+        scratch_shapes=[pltpu.VMEM((8 * leaves, lanes), f32)] + lists(3, 3 * slots_of_pairs, SENT_BATCH, False),
         cost_estimate=cost(slots_of_pairs),
         name="sent_pairs",
     )(*map(on_chip, (sub_b, corners)))
@@ -382,7 +434,7 @@
         in_specs=[vmem()] * 8,
         out_specs=vmem(),
         scratch_shapes=[pltpu.VMEM((8 * leaves, lanes), f32), pltpu.VMEM((7 * rows, lanes), f32)]
-        + lists(7, 8 * slots_of_pairs, NEAR_BATCH),
+        + lists(7, 8 * slots_of_pairs, NEAR_BATCH, True),
         cost_estimate=cost(slots_of_pairs),
         name="near_pairs",
     )(*map(on_chip, (packed, space_lower, space_upper, sub_a, sub_b, corner_a, stacks, acc)))

time: 32.9 us -> 32.3 us (0.982)
  Pallas kernels: 9.92 us -> 9.33 us
  transfers between devices with their start and end apart: 6 -> 6, of which waited for: 3 -> 3; matrix products, arithmetic and copies ran while one was open for 0% -> 0% of each run, Pallas kernels for 27% -> 25%
where the time goes in v4:
time: 32.3 us; the launch traced here: 32.1 us
  starting transfers between devices  10.7 us (33%)
  waiting for transfers between devices  10.1 us (31%)
  Pallas kernels  9.33 us (29%)
  between operations  1.37 us (4%)
  other arithmetic  0.66 us (2%)
    ppermute x4, starting transfers between devices, swapped(): return lax.ppermute(value, axis, pairs + [(j, i) for i, j in pairs])  6.67 us
    ppermute x1, waiting for transfers between devices, both_ways(): lower = lax.ppermute(value, axis, ring(size, 1))  4.37 us
    pallas_call x1, Pallas kernels, local(): pl.pallas_call(functools.partial(near_kernel, **sizes), out_shape=force,...  4.25 us
    ppermute x4, waiting for transfers between devices, swapped(): return lax.ppermute(value, axis, pairs + [(j, i) for i, j in pairs])  3.41 us
    ppermute x1, starting transfers between devices, both_ways(): lower = lax.ppermute(value, axis, ring(size, 1))  3.02 us
    pallas_call x1, Pallas kernels, local(): pl.pallas_call(functools.partial(self_kernel, leaves=leaves), out_shape=(...  2.43 us
    ppermute x1, waiting for transfers between devices, both_ways(): upper = lax.ppermute(value, axis, ring(size, -1))  2.28 us
    pallas_call x1, Pallas kernels, local(): pl.pallas_call(functools.partial(sent_kernel, **sizes), out_shape=force,...  1.4 us
  transfers between devices with their start and end apart: 6, of which 3 were waited for; matrix products, arithmetic and copies ran while one was open for 0% of the time, Pallas kernels for 25%

profile of v4, /device:TPU:0, one launch (start us, length us, event | category | flops | bytes accessed | tf_op | source)
XLA Modules:
  0.0 32.1 jit_solution(17624534563032362504)
XLA Ops:
  1.3 1.2 %pack.1.own = f32[264,128]{1,0:T(8,128)S(1)} custom-call(f32[3,1,64,128]{3,2,1,0:T(8,128)} %pos.1, f32[1,64,128]{2,1,0:T(8,128)} %mass.1, s32[1,64]{1,0:T(1,128)} %occupancy.1, s32[1,32]{1,0:T(1,128)} %slots.1, s32[2,1,64]{2,1,0:T(1,128)} %pairs.1, s32[1,128]{1,0:T(1,128)S(1)} %compare_select_fusion.counts), custom_call_target="tpu_custom_call" | custom-call | tf_op jit(solution)/shard_map/pack/pallas_call | solution.py:371
  2.6 3.0 %collective-permute-start = (f32[264,128]{1,0:T(8,128)S(1)}, f32[264,128]{1,0:T(8,128)S(1)}, u32[]{:S(2)}, u32[]{:S(2)}) collective-permute-start(f32[264,128]{1,0:T(8,128)S(1)} %pack.1.own), channel_id=1, source_target_pairs={{0,8},{8,16},{16,24},{24,0},{1,9},{9,17},{17,25},{25,1},{2,10},{10... | collective-permute-start | bytes 405512 | tf_op jit(solution)/shard_map/ppermute | solution.py:352
  5.6 1.0 %collective-permute-start.1 = (f32[264,128]{1,0:T(8,128)S(1)}, f32[264,128]{1,0:T(8,128)S(1)}, u32[]{:S(2)}, u32[]{:S(2)}) collective-permute-start(f32[264,128]{1,0:T(8,128)S(1)} %pack.1.own), channel_id=1, source_target_pairs={{0,24},{8,0},{16,8},{24,16},{1,25},{9,1},{17,9},{25,17},{2,26},{10... | collective-permute-start | bytes 405512 | tf_op jit(solution)/shard_map/ppermute | solution.py:353
  6.6 4.4 %collective-permute-done.space_lower = f32[264,128]{1,0:T(8,128)S(1)} collective-permute-done((f32[264,128]{1,0:T(8,128)S(1)}, f32[264,128]{1,0:T(8,128)S(1)}, u32[]{:S(2)}, u32[]{:S(2)}) %collective-permute-start) | collective-permute-done | bytes 135200 | tf_op jit(solution)/shard_map/ppermute | solution.py:352
  11.0 2.3 %collective-permute-done.1.space_upper = f32[264,128]{1,0:T(8,128)S(1)} collective-permute-done((f32[264,128]{1,0:T(8,128)S(1)}, f32[264,128]{1,0:T(8,128)S(1)}, u32[]{:S(2)}, u32[]{:S(2)}) %collective-permute-start.1) | collective-permute-done | bytes 135200 | tf_op jit(solution)/shard_map/ppermute | solution.py:353
  13.3 0.1 collective-permute-start.4
  13.4 3.7 %collective-permute-start.3 = (f32[264,128]{1,0:T(8,128)S(1)}, f32[264,128]{1,0:T(8,128)S(1)}, u32[]{:S(2)}, u32[]{:S(2)}) collective-permute-start(f32[264,128]{1,0:T(8,128)S(1)} %pack.1.own), channel_id=1, source_target_pairs={{1,2},{3,4},{5,6},{7,0},{2,1},{4,3},{6,5},{0,7},{9,10},{11,12},{13... | collective-permute-start | bytes 405512 | tf_op jit(solution)/shard_map/ppermute | solution.py:360
  17.1 0.0 collective-permute-start.2
  17.1 3.4 %collective-permute-done.3.sub_b = f32[264,128]{1,0:T(8,128)S(1)} collective-permute-done((f32[264,128]{1,0:T(8,128)S(1)}, f32[264,128]{1,0:T(8,128)S(1)}, u32[]{:S(2)}, u32[]{:S(2)}) %collective-permute-start.3) | collective-permute-done | bytes 135200 | tf_op jit(solution)/shard_map/ppermute | solution.py:360
  20.5 1.4 %sent_pairs.1 = f32[3,64,128]{2,1,0:T(8,128)S(1)} custom-call(f32[264,128]{1,0:T(8,128)S(1)} %collective-permute-done.3.sub_b, f32[528,128]{1,0:T(8,128)S(1)} %constant_dynamic-update-slice_fusion.corners), custom_call_target="tpu_custom_call" | custom-call | flops 209715200 | bytes 135168 | tf_op jit(solution)/shard_map/sent_pairs/pallas_call | solution.py:421
  21.9 2.9 %collective-permute-start.5 = (f32[3,64,128]{2,1,0:T(8,128)S(1)}, f32[3,64,128]{2,1,0:T(8,128)S(1)}, u32[]{:S(2)}, u32[]{:S(2)}) collective-permute-start(f32[3,64,128]{2,1,0:T(8,128)S(1)} %sent_pairs.1), channel_id=1, source_target_pairs={{1,2},{3,4},{5,6},{7,0},{2,1},{4,3},{6,5},{0,7},{9,10},{11,12},{13... | collective-permute-start | bytes 294920 | tf_op jit(solution)/shard_map/ppermute | solution.py:360
  24.8 2.4 %self_pairs.1 = (f32[512,128]{1,0:T(8,128)S(1)}, bf16[64,48,128]{2,1,0:T(8,128)(2,1)S(1)}) custom-call(f32[264,128]{1,0:T(8,128)S(1)} %pack.1.own), custom_call_target="tpu_custom_call" | custom-call | flops 209715200 | bytes 135168 | tf_op jit(solution)/shard_map/self_pairs/pallas_call | solution.py:410
  27.2 0.0 collective-permute-done.2.sub_a
  27.2 0.0 collective-permute-done.4.corner_a
  27.2 4.3 %near_pairs.1 = f32[3,64,128]{2,1,0:T(8,128)S(1)} custom-call(f32[264,128]{1,0:T(8,128)S(1)} %pack.1.own, f32[264,128]{1,0:T(8,128)S(1)} %collective-permute-done.space_lower, f32[264,128]{1,0:T(8,128)S(1)} %collective-permute-done.1.space_upper, f32[264,128]{1,0:T(8,128)S(1)} %collective-permute-done.2.sub_a, f32[264,128]{1,0:T(8,128)S(1)} %collective-permute-done.3.sub_b, ...), custom_call_target="tpu_custom_call" | custom-call | flops 209715200 | bytes 135168 | tf_op jit(solution)/shard_map/near_pairs/pallas_call | solution.py:431
  31.5 0.0 collective-permute-done.5
  31.5 0.7 %add_bitcast_fusion = f32[3,1,64,128]{3,2,1,0:T(8,128)} fusion(f32[3,64,128]{2,1,0:T(8,128)S(1)} %near_pairs.1, f32[3,64,128]{2,1,0:T(8,128)S(1)} %collective-permute-done.5), kind=kLoop, calls=%fused_computation | loop fusion | flops 24576 | bytes 294912 | tf_op jit(solution)/shard_map/broadcast_in_dim | solution.py:441
  (3 shorter events, 0.0 us)
Async XLA Ops:
  2.6 8.4 %collective-permute-start = (f32[264,128]{1,0:T(8,128)S(1)}, f32[264,128]{1,0:T(8,128)S(1)}, u32[]{:S(2)}, u32[]{:S(2)}) collective-permute-start(f32[264,128]{1,0:T(8,128)S(1)} %pack.1.own), channel_id=1, source_target_pairs={{0,8},{8,16},{16,24},{24,0},{1,9},{9,17},{17,25},{25,1},{2,10},{10... | collective-permute-start | bytes 405512 | tf_op jit(solution)/shard_map/ppermute | solution.py:352
  5.6 7.7 %collective-permute-start.1 = (f32[264,128]{1,0:T(8,128)S(1)}, f32[264,128]{1,0:T(8,128)S(1)}, u32[]{:S(2)}, u32[]{:S(2)}) collective-permute-start(f32[264,128]{1,0:T(8,128)S(1)} %pack.1.own), channel_id=1, source_target_pairs={{0,24},{8,0},{16,8},{24,16},{1,25},{9,1},{17,9},{25,17},{2,26},{10... | collective-permute-start | bytes 405512 | tf_op jit(solution)/shard_map/ppermute | solution.py:353
  13.3 13.9 %collective-permute-start.4 = (f32[528,128]{1,0:T(8,128)S(1)}, f32[528,128]{1,0:T(8,128)S(1)}, u32[]{:S(2)}, u32[]{:S(2)}) collective-permute-start(f32[528,128]{1,0:T(8,128)S(1)} %constant_dynamic-update-slice_fusion.corners), channel_id=1, source_target_pairs={{0,1},{2,3},{4,5},{6,7},{1,0},{3,2},{5,4},{7,6},{8,9},{10,11},{12,... | collective-permute-start | bytes 811016 | tf_op jit(solution)/shard_map/ppermute | solution.py:360
  13.4 7.1 %collective-permute-start.3 = (f32[264,128]{1,0:T(8,128)S(1)}, f32[264,128]{1,0:T(8,128)S(1)}, u32[]{:S(2)}, u32[]{:S(2)}) collective-permute-start(f32[264,128]{1,0:T(8,128)S(1)} %pack.1.own), channel_id=1, source_target_pairs={{1,2},{3,4},{5,6},{7,0},{2,1},{4,3},{6,5},{0,7},{9,10},{11,12},{13... | collective-permute-start | bytes 405512 | tf_op jit(solution)/shard_map/ppermute | solution.py:360
  17.1 10.1 %collective-permute-start.2 = (f32[264,128]{1,0:T(8,128)S(1)}, f32[264,128]{1,0:T(8,128)S(1)}, u32[]{:S(2)}, u32[]{:S(2)}) collective-permute-start(f32[264,128]{1,0:T(8,128)S(1)} %pack.1.own), channel_id=1, source_target_pairs={{0,1},{2,3},{4,5},{6,7},{1,0},{3,2},{5,4},{7,6},{8,9},{10,11},{12,... | collective-permute-start | bytes 405512 | tf_op jit(solution)/shard_map/ppermute | solution.py:360
  21.9 9.6 %collective-permute-start.5 = (f32[3,64,128]{2,1,0:T(8,128)S(1)}, f32[3,64,128]{2,1,0:T(8,128)S(1)}, u32[]{:S(2)}, u32[]{:S(2)}) collective-permute-start(f32[3,64,128]{2,1,0:T(8,128)S(1)} %sent_pairs.1), channel_id=1, source_target_pairs={{1,2},{3,4},{5,6},{7,0},{2,1},{4,3},{6,5},{0,7},{9,10},{11,12},{13... | collective-permute-start | bytes 294920 | tf_op jit(solution)/shard_map/ppermute | solution.py:360

commit v5 on v4

--- a/solution.py
+++ b/solution.py
@@ -13,7 +13,7 @@
 CENTER = 0.75
 TABLE = 8
 CODE = 1024
-SELF_BATCH, NEAR_BATCH, SENT_BATCH = 16, 8, 8
+OWN_BATCH, NEAR_BATCH, SENT_BATCH = 16, 8, 8
 CHUNK = 4
 
 
@@ -232,6 +232,23 @@
     return lax.fori_loop(0, lax.shift_right_logical(end - begin + (CHUNK - 1), CHUNK.bit_length() - 1), step, total)
 
 
+def append_local(tables, wanted, targets, sources, total, sent, pairs):
+    at_local = table_places(pairs, sent)[1] + LOCAL
+
+    def both(j, n):
+        code = tables[0, j]
+        t = lax.shift_right_logical(code, CODE.bit_length() - 1)
+        u = code & (CODE - 1)
+        targets[n] = t
+        sources[n] = 4 * u
+        targets[n + 1] = u
+        sources[n + 1] = 4 * t
+        return n + 2
+
+    begin = tables[0, at_local]
+    return lax.fori_loop(begin, jnp.where(wanted, tables[0, at_local + 1], begin), both, total)
+
+
 def append_ghosts(tables, offsets, first, row, stride, targets, sources, total, leaves, sent, pairs):
     at_slots, at_starts = table_places(pairs, sent)
     bits = CODE.bit_length() - 1
@@ -257,24 +274,6 @@
 
         total = append(tables[first + n, at_starts + back], tables[first + n, at_starts + back + 1], theirs, targets, sources, total)
     return total
-
-
-def self_kernel(own, acc, stacks, squares, weights, factor, moments, *, leaves):
-    acc[...] = jnp.zeros_like(acc)
-    size = 2 * squares.shape[0]
-
-    def target_of(leaf):
-        stack = target_stack(own[pl.ds(4 * leaf, 8), :])
-        stacks[leaf] = stack
-        return stack
-
-    run_pairs(
-        leaves // size,
-        lambda i, u: i * size + u,
-        lambda i, u: 4 * (i * size + u),
-        target_of,
-        own, acc, squares, weights, factor, moments,
-    )
 
 
 def fetch_tables(parts, staging, tables, sem):
@@ -283,6 +282,24 @@
     copy = pltpu.make_async_copy(staging, tables, sem)
     copy.start()
     return copy
+
+
+def own_kernel(own, acc, stacks, staging, tables, targets, sources, squares, weights, factor, moments, sem, *, leaves, sent, pairs, index_of):
+    rows = 4 * leaves
+    copy = fetch_tables([(own, rows)], staging, tables, sem)
+    acc[...] = jnp.zeros_like(acc)
+    for leaf in range(leaves):
+        targets[leaf] = leaf
+        sources[leaf] = 4 * leaf
+    copy.wait()
+    total = append_local(tables, index_of() == 0, targets, sources, leaves, sent, pairs)
+
+    def target_of(leaf):
+        stack = target_stack(own[pl.ds(4 * leaf, 8), :])
+        stacks[leaf] = stack
+        return stack
+
+    run_list(targets, sources, total, rows, target_of, own, acc, squares, weights, factor, moments)
 
 
 def forces(acc, packed, leaves):
@@ -315,7 +332,8 @@
 def near_kernel(own, space_lower, space_upper, sub_a, sub_b, corner_a, stacks, acc_in, out, acc, pool, staging, tables, targets, sources, squares, weights, factor, moments, sem, *, leaves, sent, pairs, index_of):
     rows = 4 * leaves
     stride = rows + TABLE
-    odd = lax.rem(index_of(), 2)
+    index = index_of()
+    odd = lax.rem(index, 2)
     parts = [(own, 0), (space_lower, 0), (space_upper, 0), (sub_a, 0), (sub_b, 0), (corner_a, 0), (corner_a, stride)]
     copy = fetch_tables([(ref, row + rows) for ref, row in parts], staging, tables, sem)
     acc[...] = acc_in[...]
@@ -323,19 +341,7 @@
         pool[pl.ds(n * stride, stride), :] = ref[pl.ds(row, stride), :]
     copy.wait()
 
-    at_starts = table_places(pairs, sent)[1]
-
-    def both(j, n):
-        code = tables[0, j]
-        t = lax.shift_right_logical(code, CODE.bit_length() - 1)
-        u = code & (CODE - 1)
-        targets[n] = t
-        sources[n] = 4 * u
-        targets[n + 1] = u
-        sources[n + 1] = 4 * t
-        return n + 2
-
-    total = lax.fori_loop(tables[0, at_starts + LOCAL], tables[0, at_starts + LOCAL + 1], both, 0)
+    total = append_local(tables, index != 0, targets, sources, 0, sent, pairs)
     offsets = (1, 6, 4 - odd, 3 + odd, 2 - 2 * odd, 7 - 2 * odd)
     total = append_ghosts(tables, offsets, 1, stride, stride, targets, sources, total, leaves, sent, pairs)
     run_list(targets, sources, total, rows, lambda leaf: stacks[leaf], pool, acc, squares, weights, factor, moments)
@@ -408,13 +414,13 @@
     sub_a = swapped(packed, "sub", 0)
     sub_b = swapped(packed, "sub", 1)
     acc, stacks = pl.pallas_call(
-        functools.partial(self_kernel, leaves=leaves),
+        functools.partial(own_kernel, **sizes),
         out_shape=(accumulator, pltpu.VMEM((leaves, STACK, lanes), jnp.bfloat16)),
         in_specs=[vmem()],
         out_specs=(vmem(), vmem()),
-        scratch_shapes=pairing(SELF_BATCH, True),
+        scratch_shapes=lists(1, leaves + 2 * slots_of_pairs, OWN_BATCH, True),
         cost_estimate=cost(leaves),
-        name="self_pairs",
+        name="own_pairs",
     )(on_chip(packed))
     corners = jnp.concatenate([space_lower, space_upper], axis=0)
     corner_a = swapped(corners, "sub", 0)

time: 32.3 us -> 33 us (1.022)
  Pallas kernels: 9.33 us -> 10 us
    pallas_call x1, Pallas kernels: 2.43 us -> 4.23 us  [local(): pl.pallas_call(functools.partial(own_kernel, **sizes), out_shape=(accumul...]
    pallas_call x1, Pallas kernels: 4.25 us -> 3.14 us  [local(): pl.pallas_call(functools.partial(near_kernel, **sizes), out_shape=force,...]
  transfers between devices with their start and end apart: 6 -> 6, of which waited for: 3 -> 3; matrix products, arithmetic and copies ran while one was open for 0% -> 0% of each run, Pallas kernels for 25% -> 27%
where the time goes in v5:
time: 33 us; the launch traced here: 32.8 us
  starting transfers between devices  10.7 us (32%)
  waiting for transfers between devices  10.1 us (31%)
  Pallas kernels  10 us (30%)
  between operations  1.38 us (4%)
  other arithmetic  0.66 us (2%)
    ppermute x4, starting transfers between devices, swapped(): return lax.ppermute(value, axis, pairs + [(j, i) for i, j in pairs])  6.67 us
    ppermute x1, waiting for transfers between devices, both_ways(): lower = lax.ppermute(value, axis, ring(size, 1))  4.37 us
    pallas_call x1, Pallas kernels, local(): pl.pallas_call(functools.partial(own_kernel, **sizes), out_shape=(accumul...  4.23 us
    ppermute x4, waiting for transfers between devices, swapped(): return lax.ppermute(value, axis, pairs + [(j, i) for i, j in pairs])  3.4 us
    pallas_call x1, Pallas kernels, local(): pl.pallas_call(functools.partial(near_kernel, **sizes), out_shape=force,...  3.14 us
    ppermute x1, starting transfers between devices, both_ways(): lower = lax.ppermute(value, axis, ring(size, 1))  3.02 us
    ppermute x1, waiting for transfers between devices, both_ways(): upper = lax.ppermute(value, axis, ring(size, -1))  2.28 us
    pallas_call x1, Pallas kernels, local(): pl.pallas_call(functools.partial(sent_kernel, **sizes), out_shape=force,...  1.4 us
  transfers between devices with their start and end apart: 6, of which 3 were waited for; matrix products, arithmetic and copies ran while one was open for 0% of the time, Pallas kernels for 27%

profile of v5, /device:TPU:0, one launch (start us, length us, event | category | flops | bytes accessed | tf_op | source)
XLA Modules:
  0.0 32.8 jit_solution(306777614368609898)
XLA Ops:
  1.3 1.2 %pack.1.own = f32[264,128]{1,0:T(8,128)S(1)} custom-call(f32[3,1,64,128]{3,2,1,0:T(8,128)} %pos.1, f32[1,64,128]{2,1,0:T(8,128)} %mass.1, s32[1,64]{1,0:T(1,128)} %occupancy.1, s32[1,32]{1,0:T(1,128)} %slots.1, s32[2,1,64]{2,1,0:T(1,128)} %pairs.1, s32[1,128]{1,0:T(1,128)S(1)} %compare_select_fusion.counts), custom_call_target="tpu_custom_call" | custom-call | tf_op jit(solution)/shard_map/pack/pallas_call | solution.py:377
  2.6 3.0 %collective-permute-start = (f32[264,128]{1,0:T(8,128)S(1)}, f32[264,128]{1,0:T(8,128)S(1)}, u32[]{:S(2)}, u32[]{:S(2)}) collective-permute-start(f32[264,128]{1,0:T(8,128)S(1)} %pack.1.own), channel_id=1, source_target_pairs={{0,8},{8,16},{16,24},{24,0},{1,9},{9,17},{17,25},{25,1},{2,10},{10... | collective-permute-start | bytes 405512 | tf_op jit(solution)/shard_map/ppermute | solution.py:358
  5.6 1.0 %collective-permute-start.1 = (f32[264,128]{1,0:T(8,128)S(1)}, f32[264,128]{1,0:T(8,128)S(1)}, u32[]{:S(2)}, u32[]{:S(2)}) collective-permute-start(f32[264,128]{1,0:T(8,128)S(1)} %pack.1.own), channel_id=1, source_target_pairs={{0,24},{8,0},{16,8},{24,16},{1,25},{9,1},{17,9},{25,17},{2,26},{10... | collective-permute-start | bytes 405512 | tf_op jit(solution)/shard_map/ppermute | solution.py:359
  6.6 4.4 %collective-permute-done.space_lower = f32[264,128]{1,0:T(8,128)S(1)} collective-permute-done((f32[264,128]{1,0:T(8,128)S(1)}, f32[264,128]{1,0:T(8,128)S(1)}, u32[]{:S(2)}, u32[]{:S(2)}) %collective-permute-start) | collective-permute-done | bytes 135200 | tf_op jit(solution)/shard_map/ppermute | solution.py:358
  11.0 2.3 %collective-permute-done.1.space_upper = f32[264,128]{1,0:T(8,128)S(1)} collective-permute-done((f32[264,128]{1,0:T(8,128)S(1)}, f32[264,128]{1,0:T(8,128)S(1)}, u32[]{:S(2)}, u32[]{:S(2)}) %collective-permute-start.1) | collective-permute-done | bytes 135200 | tf_op jit(solution)/shard_map/ppermute | solution.py:359
  13.3 0.1 collective-permute-start.4
  13.4 3.7 %collective-permute-start.3 = (f32[264,128]{1,0:T(8,128)S(1)}, f32[264,128]{1,0:T(8,128)S(1)}, u32[]{:S(2)}, u32[]{:S(2)}) collective-permute-start(f32[264,128]{1,0:T(8,128)S(1)} %pack.1.own), channel_id=1, source_target_pairs={{1,2},{3,4},{5,6},{7,0},{2,1},{4,3},{6,5},{0,7},{9,10},{11,12},{13... | collective-permute-start | bytes 405512 | tf_op jit(solution)/shard_map/ppermute | solution.py:366
  17.1 0.0 collective-permute-start.2
  17.1 3.4 %collective-permute-done.3.sub_b = f32[264,128]{1,0:T(8,128)S(1)} collective-permute-done((f32[264,128]{1,0:T(8,128)S(1)}, f32[264,128]{1,0:T(8,128)S(1)}, u32[]{:S(2)}, u32[]{:S(2)}) %collective-permute-start.3) | collective-permute-done | bytes 135200 | tf_op jit(solution)/shard_map/ppermute | solution.py:366
  20.5 1.4 %sent_pairs.1 = f32[3,64,128]{2,1,0:T(8,128)S(1)} custom-call(f32[264,128]{1,0:T(8,128)S(1)} %collective-permute-done.3.sub_b, f32[528,128]{1,0:T(8,128)S(1)} %constant_dynamic-update-slice_fusion.corners), custom_call_target="tpu_custom_call" | custom-call | flops 209715200 | bytes 135168 | tf_op jit(solution)/shard_map/sent_pairs/pallas_call | solution.py:427
  21.9 2.9 %collective-permute-start.5 = (f32[3,64,128]{2,1,0:T(8,128)S(1)}, f32[3,64,128]{2,1,0:T(8,128)S(1)}, u32[]{:S(2)}, u32[]{:S(2)}) collective-permute-start(f32[3,64,128]{2,1,0:T(8,128)S(1)} %sent_pairs.1), channel_id=1, source_target_pairs={{1,2},{3,4},{5,6},{7,0},{2,1},{4,3},{6,5},{0,7},{9,10},{11,12},{13... | collective-permute-start | bytes 294920 | tf_op jit(solution)/shard_map/ppermute | solution.py:366
  24.8 4.2 %own_pairs.1 = (f32[512,128]{1,0:T(8,128)S(1)}, bf16[64,48,128]{2,1,0:T(8,128)(2,1)S(1)}) custom-call(f32[264,128]{1,0:T(8,128)S(1)} %pack.1.own), custom_call_target="tpu_custom_call" | custom-call | flops 209715200 | bytes 135168 | tf_op jit(solution)/shard_map/own_pairs/pallas_call | solution.py:416
  29.0 0.0 collective-permute-done.2.sub_a
  29.0 0.0 collective-permute-done.4.corner_a
  29.0 3.1 %near_pairs.1 = f32[3,64,128]{2,1,0:T(8,128)S(1)} custom-call(f32[264,128]{1,0:T(8,128)S(1)} %pack.1.own, f32[264,128]{1,0:T(8,128)S(1)} %collective-permute-done.space_lower, f32[264,128]{1,0:T(8,128)S(1)} %collective-permute-done.1.space_upper, f32[264,128]{1,0:T(8,128)S(1)} %collective-permute-done.2.sub_a, f32[264,128]{1,0:T(8,128)S(1)} %collective-permute-done.3.sub_b, ...), custom_call_target="tpu_custom_call" | custom-call | flops 209715200 | bytes 135168 | tf_op jit(solution)/shard_map/near_pairs/pallas_call | solution.py:437
  32.2 0.0 collective-permute-done.5
  32.2 0.7 %add_bitcast_fusion = f32[3,1,64,128]{3,2,1,0:T(8,128)} fusion(f32[3,64,128]{2,1,0:T(8,128)S(1)} %near_pairs.1, f32[3,64,128]{2,1,0:T(8,128)S(1)} %collective-permute-done.5), kind=kLoop, calls=%fused_computation | loop fusion | flops 24576 | bytes 294912 | tf_op jit(solution)/shard_map/broadcast_in_dim | solution.py:447
  (3 shorter events, 0.0 us)
Async XLA Ops:
  2.6 8.4 %collective-permute-start = (f32[264,128]{1,0:T(8,128)S(1)}, f32[264,128]{1,0:T(8,128)S(1)}, u32[]{:S(2)}, u32[]{:S(2)}) collective-permute-start(f32[264,128]{1,0:T(8,128)S(1)} %pack.1.own), channel_id=1, source_target_pairs={{0,8},{8,16},{16,24},{24,0},{1,9},{9,17},{17,25},{25,1},{2,10},{10... | collective-permute-start | bytes 405512 | tf_op jit(solution)/shard_map/ppermute | solution.py:358
  5.6 7.7 %collective-permute-start.1 = (f32[264,128]{1,0:T(8,128)S(1)}, f32[264,128]{1,0:T(8,128)S(1)}, u32[]{:S(2)}, u32[]{:S(2)}) collective-permute-start(f32[264,128]{1,0:T(8,128)S(1)} %pack.1.own), channel_id=1, source_target_pairs={{0,24},{8,0},{16,8},{24,16},{1,25},{9,1},{17,9},{25,17},{2,26},{10... | collective-permute-start | bytes 405512 | tf_op jit(solution)/shard_map/ppermute | solution.py:359
  13.3 15.7 %collective-permute-start.4 = (f32[528,128]{1,0:T(8,128)S(1)}, f32[528,128]{1,0:T(8,128)S(1)}, u32[]{:S(2)}, u32[]{:S(2)}) collective-permute-start(f32[528,128]{1,0:T(8,128)S(1)} %constant_dynamic-update-slice_fusion.corners), channel_id=1, source_target_pairs={{0,1},{2,3},{4,5},{6,7},{1,0},{3,2},{5,4},{7,6},{8,9},{10,11},{12,... | collective-permute-start | bytes 811016 | tf_op jit(solution)/shard_map/ppermute | solution.py:366
  13.4 7.1 %collective-permute-start.3 = (f32[264,128]{1,0:T(8,128)S(1)}, f32[264,128]{1,0:T(8,128)S(1)}, u32[]{:S(2)}, u32[]{:S(2)}) collective-permute-start(f32[264,128]{1,0:T(8,128)S(1)} %pack.1.own), channel_id=1, source_target_pairs={{1,2},{3,4},{5,6},{7,0},{2,1},{4,3},{6,5},{0,7},{9,10},{11,12},{13... | collective-permute-start | bytes 405512 | tf_op jit(solution)/shard_map/ppermute | solution.py:366
  17.1 11.9 %collective-permute-start.2 = (f32[264,128]{1,0:T(8,128)S(1)}, f32[264,128]{1,0:T(8,128)S(1)}, u32[]{:S(2)}, u32[]{:S(2)}) collective-permute-start(f32[264,128]{1,0:T(8,128)S(1)} %pack.1.own), channel_id=1, source_target_pairs={{0,1},{2,3},{4,5},{6,7},{1,0},{3,2},{5,4},{7,6},{8,9},{10,11},{12,... | collective-permute-start | bytes 405512 | tf_op jit(solution)/shard_map/ppermute | solution.py:366
  21.9 10.3 %collective-permute-start.5 = (f32[3,64,128]{2,1,0:T(8,128)S(1)}, f32[3,64,128]{2,1,0:T(8,128)S(1)}, u32[]{:S(2)}, u32[]{:S(2)}) collective-permute-start(f32[3,64,128]{2,1,0:T(8,128)S(1)} %sent_pairs.1), channel_id=1, source_target_pairs={{1,2},{3,4},{5,6},{7,0},{2,1},{4,3},{6,5},{0,7},{9,10},{11,12},{13... | collective-permute-start | bytes 294920 | tf_op jit(solution)/shard_map/ppermute | solution.py:366
